TPU v7x, 32 devices: a whole 2x2x4 slice. The times are simulated.
32 devices in a mesh: group: 4 (over z), sub: 8 (over y, x, core).
Axes of the slice: x: 2, y: 2, z: 4, core: 2. Of those that a mesh axis runs over, the one named last changes fastest.
Arguments:
- displacement: float32 [3, 35, 32768], P(None, None, ('group', 'sub')), may hold values from -6 to 6
- velocity: float32 [3, 35, 32768], P(None, None, ('group', 'sub')), may hold values from -6 to 6
- geometry_weights: float32 [6, 32768], P(None, ('group', 'sub')), may hold values from 0.2 to 2
- jacobian: float32 [32768], P(('group', 'sub')), may hold values from 0.5 to 2
- strain_map: float32 [630, 105], replicated, may hold values from -0.25 to 0.25
- face_mass: float32 [15, 15], replicated, may hold values from -1 to 2, as said below
- mass_inverse: float32 [35, 35], replicated, may hold values from -1 to 2, as said below
- local_links: int32 [2, 98304], P(None, ('group', 'sub')), may hold values from 0 to 383, as said below
- local_geometry: float32 [4, 98304], P(None, ('group', 'sub')), may hold values from -1 to 3, as said below
- neighbour_links: int32 [2, 4096], P(None, ('group', 'sub')), may hold values from 0 to 2, as said below
- neighbour_geometry: float32 [8, 4096], P(None, ('group', 'sub')), may hold values from -1 to 3, as said below
- cross_links: int32 [6144], P(('group', 'sub')), may hold values from 0 to 2, as said below
- cross_geometry: float32 [4, 6144], P(None, ('group', 'sub')), may hold values from -1 to 3, as said below
Outputs:
- displacement_new: float32 [3, 35, 32768], P(None, None, ('group', 'sub'))
- velocity_new: float32 [3, 35, 32768], P(None, None, ('group', 'sub'))
Inputs may be any that keep to these rules, and one draw needn't show every extreme that they name: `local_links`: row 0 is the partner inside the same aligned block of 128 elements, as the steps read it; the pairing is symmetric and never pairs a half-face with itself. Row 1 is the state (0 intact, 1 cohesive, 2 broken), equal on both half-faces of a pair. `local_geometry`: rows 0 to 2 are a unit normal, row 3 a positive scale; both half-faces of a pair hold the same values. `neighbour_links`: row 0: state of the upper shared half-face, row 1: of the lower one (0 intact, 1 cohesive, 2 broken). Row 1 of device (g, s) equals row 0 of the same column on device (g, (s - 1) mod 8). `neighbour_geometry`: rows 0 to 3: unit normal and positive scale of the upper half-face; rows 4 to 7 of device (g, s) equal rows 0 to 3 of the same column on device (g, (s - 1) mod 8). `cross_links`: states (0 intact, 1 cohesive, 2 broken). In the block of 8 slots that a device holds for one partner device, the first count slots hold faces and the rest are padding with state 2; count is the same on both sides of a pair, 1 to 8, 8 for some pair, and the states of matching slots agree. `cross_geometry`: rows 0 to 2 a unit normal, row 3 a positive scale; matching slots of a pair hold the same values. `face_mass`: Symmetric. `mass_inverse`: Symmetric.
All inputs are finite; a program needn't handle non-finite values.
Results may differ from a plain program's by a relative error of at most 0.00011.
Values sent between devices are 32-bit elements; how exact they have to be, the bound alone decides.
No kernel may reach another device: no remote copies, remote signals or barrier semaphores. Data moves between devices by JAX's collectives and lax.ppermute only.
A program may use at most 128 MiB of HBM per device.

v0:
```python
import jax
import jax.numpy as jnp
import numpy as np
from jax import lax
from jax.sharding import PartitionSpec as P

BLOCK = 128
STEPS = 5


shear_weight = 0.5
opening_scale = 4.0
time_step = 0.25
highest = lax.Precision.HIGHEST


def shifted(value, axis, steps):
    count = lax.axis_size(axis)
    pairs = [(source, (source + steps) % count) for source in range(count)]
    return lax.ppermute(value, axis, pairs)


def face_table():
    points = [
        (first, second, third, 4 - first - second - third)
        for first in range(5)
        for second in range(5 - first)
        for third in range(5 - first - second)
    ]
    result = np.zeros((4, 15, 35), np.float32)
    for side in range(4):
        members = [index for index, point in enumerate(points) if point[side] == 0]
        for place, index in enumerate(members):
            result[side, place, index] = 1.0
    return result


def cohesive_traction(jump, normal, state):
    along = jnp.sum(normal[:, None, :] * jump, axis=0)
    normal_part = along[None] * normal[:, None, :]
    tangent = jump - normal_part
    opening = along * along + shear_weight * jnp.sum(tangent * tangent, axis=0)
    softened = jnp.exp(-opening / opening_scale)[None] * (normal_part + shear_weight * tangent)
    zeros = jnp.zeros_like(jump)
    return jnp.where(
        state[None, None, :] == 0, jump, jnp.where(state[None, None, :] == 1, softened, zeros)
    )


def apply_mass(traction, scale, face_mass):
    spread = jnp.einsum("ij,cjf->cif", face_mass, traction, precision=highest)
    return scale[None, None, :] * spread


def face_force(jump, geometry, state, face_mass):
    return apply_mass(cohesive_traction(jump, geometry[0:3], state), geometry[3], face_mass)


def route_traces(blocks):
    arrived = []
    for offset in range(blocks.shape[2]):
        mixed = lax.all_to_all(blocks[:, :, offset], "sub", split_axis=2, concat_axis=2, tiled=True)
        arrived.append(shifted(mixed, "group", offset + 1))
    return jnp.stack(arrived[::-1], axis=2)


def shards(
    displacement,
    velocity,
    geometry_weights,
    jacobian,
    strain_map,
    face_mass,
    mass_inverse,
    local_links,
    local_geometry,
    neighbour_links,
    neighbour_geometry,
    cross_links,
    cross_geometry,
):
    table = jnp.asarray(face_table())
    components = displacement.shape[0]
    node_count = displacement.shape[1]
    elements = displacement.shape[2]
    face_nodes = table.shape[1]
    pieces = strain_map.shape[0] // (components * node_count)
    groups = lax.axis_size("group")
    slots = cross_links.shape[0]
    shared = neighbour_links.shape[1]
    width = slots // (groups - 1)
    spare = elements - 2 * shared - slots
    count_blocks = elements // BLOCK
    partner = jnp.transpose(local_links[0].reshape(3, count_blocks, BLOCK), (1, 0, 2))
    labels = (
        jnp.arange(3, dtype=jnp.int32)[:, None] * BLOCK
        + jnp.arange(BLOCK, dtype=jnp.int32)[None, :]
    )
    selector = (partner[:, None, None, :, :] == labels[None, :, :, None, None]).astype(jnp.float32)
    filler = jnp.zeros((components, face_nodes, spare), jnp.float32)
    field = displacement
    for step in range(STEPS):
        traces = jnp.einsum("kin,cne->cike", table, field, precision=highest)
        own_local = traces[:, :, 1:]
        paired = jnp.einsum(
            "cikjb,jkbql->ciqjl",
            own_local.reshape(components, face_nodes, 3, count_blocks, BLOCK),
            selector,
            precision=highest,
        )
        jump = paired.reshape(components, face_nodes, 3 * elements) - own_local.reshape(
            components, face_nodes, 3 * elements
        )
        local_force = face_force(jump, local_geometry, local_links[1], face_mass)
        rim = traces[:, :, 0]
        upper = rim[:, :, 0:shared]
        lower = rim[:, :, shared : 2 * shared]
        outgoing = rim[:, :, 2 * shared : 2 * shared + slots]
        arrived = shifted(lower, "sub", -1)
        upper_force = face_force(
            arrived - upper, neighbour_geometry[0:4], neighbour_links[0], face_mass
        )
        lower_force = -shifted(upper_force, "sub", 1)
        blocks = outgoing.reshape(components, face_nodes, groups - 1, width)
        incoming = route_traces(blocks).reshape(components, face_nodes, slots)
        cross_force = face_force(incoming - outgoing, cross_geometry, cross_links, face_mass)
        rim_force = jnp.concatenate([upper_force, lower_force, cross_force, filler], axis=2)
        forces = jnp.concatenate(
            [rim_force[:, :, None], local_force.reshape(components, face_nodes, 3, elements)],
            axis=2,
        )
        face_load = jnp.einsum("kin,cike->cne", table, forces, precision=highest)
        strain = jnp.dot(
            strain_map, field.reshape(components * node_count, elements), precision=highest
        )
        weighted = (
            strain.reshape(pieces, components * node_count, elements) * geometry_weights[:, None, :]
        ).reshape(pieces * components * node_count, elements)
        volume = -jnp.dot(strain_map.T, weighted, precision=highest).reshape(
            components, node_count, elements
        )
        acceleration = (
            jnp.einsum("nm,cme->cne", mass_inverse, volume + face_load, precision=highest)
            / jacobian[None, None, :]
        )
        velocity = velocity + time_step * acceleration
        field = field + time_step * velocity
    return (field, velocity)


def solution(mesh):
    return jax.shard_map(
        shards,
        mesh=mesh,
        in_specs=(
            P(None, None, ("group", "sub")),
            P(None, None, ("group", "sub")),
            P(None, ("group", "sub")),
            P(("group", "sub")),
            P(),
            P(),
            P(),
            P(None, ("group", "sub")),
            P(None, ("group", "sub")),
            P(None, ("group", "sub")),
            P(None, ("group", "sub")),
            P(("group", "sub")),
            P(None, ("group", "sub")),
        ),
        out_specs=(P(None, None, ("group", "sub")), P(None, None, ("group", "sub"))),
        check_vma=False,
    )
```

profile of v0, /device:TPU:0, one launch (start us, length us, event | category | flops | bytes accessed | tf_op | source)
XLA Modules:
  0.0 459.1 jit_solution(2405051628623614318)
XLA Ops:
  4.3 5.2 %all-to-all-start.2 = ((f32[8,1,360]{2,1,0:T(1,128)}), f32[8,1,360]{2,1,0:T(1,128)}, u32[]{:S(2)}, u32[]{:S(2)}) async-start(f32[8,1,360]{2,1,0:T(1,128)} %reshape.527), calls=%async_computation.2 | async-start | bytes 24576 | tf_op jit(solution)/shard_map/all_to_all | solution.py:62
  10.1 2.6 collective-permute-start
  20.9 3.3 convolution_multiply_fusion.5
  26.1 3.7 fusion.72
  33.6 3.3 all-to-all-start.1
  38.3 3.3 all-to-all-done.1
  41.6 3.3 all-to-all-start
  51.5 2.6 collective-permute-start.3
  55.6 12.4 %collective-permute-start.2 = (f32[3,15,64]{1,0,2:T(4,128)}, f32[3,15,64]{1,0,2:T(4,128)}, u32[]{:S(2)}, u32[]{:S(2)}) collective-permute-start(f32[3,15,64]{1,0,2:T(4,128)} %bitcast.400), channel_id=1, source_target_pairs={{0,24},{8,0},{16,8},{24,16},{1,25},{9,1},{17,9},{25,17},{2,26},{10... | collective-permute-start | bytes 34568 | tf_op jit(solution)/shard_map/ppermute | solution.py:20
  72.6 2.1 mul.1026
  83.8 3.1 collective-permute-done.1
  88.7 2.4 multiply_add_fusion.9
  94.4 3.7 fusion.363
  100.0 3.0 multiply_reduce_fusion.7
  114.3 3.9 all-to-all-start.5
  126.1 4.1 all-to-all-start.4
  135.1 3.9 all-to-all-start.3
  139.0 4.7 %fusion.65 = f32[105,1024]{1,0:T(8,128)} fusion(f32[630,105]{0,1:T(8,128)S(1)} %copy-done.1, f32[630,1024]{1,0:T(8,128)S(1)} %mul.1026, f32[1024,630]{0,1:T(8,128)} %fusion.363), kind=kOutput, calls=%fused_computation.80 | convolution fusion | flops 813603840 | bytes 5855640 | tf_op jit(solution)/shard_map/dot_general | solution.py:139
  147.1 2.4 reshape.476
  149.4 2.0 reduce.17
  153.6 2.0 reduce.18
  157.5 2.0 reduce.19
  161.0 2.7 collective-permute-start.7
  163.7 3.0 fusion.16
  169.8 2.4 reshape.477
  173.6 2.0 collective-permute-start.5
  185.1 3.1 collective-permute-done.6
  190.1 2.4 multiply_add_fusion.8
  195.7 3.7 fusion.364
  201.3 3.0 multiply_reduce_fusion.5
  212.1 3.3 all-to-all-start.8
  221.9 4.1 all-to-all-start.7
  230.8 3.9 all-to-all-start.6
  234.7 4.7 %fusion.67 = f32[105,1024]{1,0:T(8,128)} fusion(f32[630,105]{0,1:T(8,128)S(1)} %copy-done.1, f32[630,1024]{1,0:T(8,128)S(1)} %mul.1026, f32[1024,630]{0,1:T(8,128)} %fusion.364), kind=kOutput, calls=%fused_computation.82 | convolution fusion | flops 813603840 | bytes 5855640 | tf_op jit(solution)/shard_map/dot_general | solution.py:139
  243.6 2.3 reshape.483
  253.6 3.1 collective-permute-start.12
  256.7 3.1 fusion.17
  262.9 2.4 reshape.484
  265.3 2.3 copy.416
  277.7 3.1 collective-permute-done.11
  282.8 2.2 multiply_add_fusion.7
  289.5 3.7 fusion.365
  294.1 3.0 multiply_reduce_fusion.3
  308.4 3.9 all-to-all-start.11
  320.3 4.1 all-to-all-start.10
  329.3 3.9 all-to-all-start.9
  333.2 4.7 %fusion.69 = f32[105,1024]{1,0:T(8,128)} fusion(f32[630,105]{0,1:T(8,128)S(1)} %copy-done.1, f32[630,1024]{1,0:T(8,128)S(1)} %mul.1026, f32[1024,630]{0,1:T(8,128)} %fusion.365), kind=kOutput, calls=%fused_computation.84 | convolution fusion | flops 813603840 | bytes 5855640 | tf_op jit(solution)/shard_map/dot_general | solution.py:139
  341.2 2.4 reshape.490
  343.6 2.0 reduce.23
  347.1 2.0 reduce.24
  351.7 2.0 reduce.25
  355.2 2.9 collective-permute-start.17
  358.1 3.0 fusion.18
  364.3 2.4 reshape.491
  379.1 3.1 collective-permute-done.16
  384.1 2.4 multiply_add_fusion.6
  389.7 3.7 fusion.366
  395.3 3.0 multiply_reduce_fusion.1
  406.0 3.3 all-to-all-start.14
  415.8 4.1 all-to-all-start.13
  424.7 3.3 all-to-all-start.12
  428.0 4.7 %fusion.71 = f32[105,1024]{1,0:T(8,128)} fusion(f32[630,105]{0,1:T(8,128)S(1)} %copy-done.1, f32[630,1024]{1,0:T(8,128)S(1)} %mul.1026, f32[1024,630]{0,1:T(8,128)} %fusion.366), kind=kOutput, calls=%fused_computation.86 | convolution fusion | flops 813603840 | bytes 5855640 | tf_op jit(solution)/shard_map/dot_general | solution.py:139
  440.1 3.2 collective-permute-start.22
  452.7 3.6 collective-permute-done.21
  (486 shorter events, 246.4 us)
Async XLA Ops:
  0.6 88.1 %copy-start = (f32[35,35]{1,0:T(8,128)S(1)}, f32[35,35]{1,0:T(8,128)}, u32[]{:S(2)}) copy-start(f32[35,35]{1,0:T(8,128)} %param.20) | copy-start | bytes 14704
  0.6 12.1 %copy-start.6 = (f32[3,35,1024]{2,1,0:T(8,128)S(1)}, f32[3,35,1024]{2,1,0:T(8,128)}, u32[]{:S(2)}) copy-start(f32[3,35,1024]{2,1,0:T(8,128)} %param.14) | copy-start | bytes 1290244
  2.6 11.6 %copy-start.35 = (f32[3,15,1024]{2,1,0:T(8,128)}, f32[3,15,1024]{2,1,0:T(8,128)S(1)}, u32[]{:S(2)}) copy-start(f32[3,15,1024]{2,1,0:T(8,128)S(1)} %slice_bitcast_fusion.4) | copy-start | bytes 552964
  3.3 10.8 %copy-start.62 = (f32[4,3072]{1,0:T(4,128)S(1)}, f32[4,3072]{1,0:T(4,128)}, u32[]{:S(2)}) copy-start(f32[4,3072]{1,0:T(4,128)} %param.22) | copy-start | bytes 147460
  3.5 11.4 %slice-start.2 = ((s32[2,3072]{1,0:T(2,128)}), s32[1,3072]{1,0:T(1,128)S(1)}, s32[]{:S(2)}) async-start(s32[2,3072]{1,0:T(2,128)} %param.21), calls=%async_computation.17 | async-start | bytes 24576 | tf_op jit(solution)/shard_map/slice | solution.py:94
  4.3 29.4 %all-to-all-start.2 = ((f32[8,1,360]{2,1,0:T(1,128)}), f32[8,1,360]{2,1,0:T(1,128)}, u32[]{:S(2)}, u32[]{:S(2)}) async-start(f32[8,1,360]{2,1,0:T(1,128)} %reshape.527), calls=%async_computation.2 | async-start | bytes 24576 | tf_op jit(solution)/shard_map/all_to_all | solution.py:62
  10.1 70.1 %collective-permute-start = (f32[3,15,128]{2,1,0:T(8,128)}, f32[3,15,128]{2,1,0:T(8,128)}, u32[]{:S(2)}, u32[]{:S(2)}) collective-permute-start(f32[3,15,128]{2,1,0:T(8,128)} %slice.236), channel_id=1, source_target_pairs={{0,7},{1,0},{2,1},{3,2},{4,3},{5,4},{6,5},{7,6},{8,15},{9,8},{10,9... | collective-permute-start | bytes 69128 | tf_op jit(solution)/shard_map/ppermute | solution.py:20
  19.3 12.6 %copy-start.47 = (f32[1,3072]{1,0:T(1,128)}, f32[1,3072]{1,0:T(1,128)S(1)}, u32[]{:S(2)}) copy-start(f32[1,3072]{1,0:T(1,128)S(1)} %slice.198) | copy-start | bytes 36868
  30.4 14.6 %copy-start.78 = (s32[192]{0:T(256)S(1)}, s32[192]{0:T(256)}, u32[]{:S(2)}) copy-start(s32[192]{0:T(256)} %param.25) | copy-start | bytes 2308
  31.4 36.6 %copy-start.79 = (s32[2,128]{1,0:T(2,128)S(1)}, s32[2,128]{1,0:T(2,128)}, u32[]{:S(2)}) copy-start(s32[2,128]{1,0:T(2,128)} %param.23) | copy-start | bytes 3076
  32.8 37.3 %copy-start.37 = (f32[4,192]{1,0:T(4,128)S(1)}, f32[4,192]{1,0:T(4,128)}, u32[]{:S(2)}) copy-start(f32[4,192]{1,0:T(4,128)} %param.26) | copy-start | bytes 9220
  32.8 37.9 %copy-start.50 = (f32[6,1024]{1,0:T(8,128)S(1)}, f32[6,1024]{1,0:T(8,128)}, u32[]{:S(2)}) copy-start(f32[6,1024]{1,0:T(8,128)} %param.16) | copy-start | bytes 73732
  33.6 8.0 %all-to-all-start.1 = ((f32[8,1,360]{2,1,0:T(1,128)}), f32[8,1,360]{2,1,0:T(1,128)S(1)}, u32[]{:S(2)}, u32[]{:S(2)}) async-start(f32[8,1,360]{2,1,0:T(1,128)} %reshape.529), calls=%async_computation.1 | async-start | bytes 24576 | tf_op jit(solution)/shard_map/all_to_all | solution.py:62
  41.6 12.5 %all-to-all-start = ((f32[8,1,360]{2,1,0:T(1,128)}), f32[8,1,360]{2,1,0:T(1,128)S(1)}, u32[]{:S(2)}, u32[]{:S(2)}) async-start(f32[8,1,360]{2,1,0:T(1,128)} %reshape.531), calls=%async_computation | async-start | bytes 24576 | tf_op jit(solution)/shard_map/all_to_all | solution.py:62
  48.4 26.4 %collective-permute-start.4 = (f32[3,15,64]{1,0,2:T(4,128)}, f32[3,15,64]{1,0,2:T(4,128)}, u32[]{:S(2)}, u32[]{:S(2)}) collective-permute-start(f32[3,15,64]{1,0,2:T(4,128)} %bitcast.396), channel_id=1, source_target_pairs={{0,8},{8,16},{16,24},{24,0},{1,9},{9,17},{17,25},{25,1},{2,10},{10... | collective-permute-start | bytes 34568 | tf_op jit(solution)/shard_map/ppermute | solution.py:20
  51.5 23.2 %collective-permute-start.3 = (f32[3,15,64]{1,0,2:T(4,128)}, f32[3,15,64]{1,0,2:T(4,128)}, u32[]{:S(2)}, u32[]{:S(2)}) collective-permute-start(f32[3,15,64]{1,0,2:T(4,128)} %bitcast.398), channel_id=1, source_target_pairs={{0,16},{8,24},{16,0},{24,8},{1,17},{9,25},{17,1},{25,9},{2,18},{10... | collective-permute-start | bytes 34568 | tf_op jit(solution)/shard_map/ppermute | solution.py:20
  55.6 19.1 %collective-permute-start.2 = (f32[3,15,64]{1,0,2:T(4,128)}, f32[3,15,64]{1,0,2:T(4,128)}, u32[]{:S(2)}, u32[]{:S(2)}) collective-permute-start(f32[3,15,64]{1,0,2:T(4,128)} %bitcast.400), channel_id=1, source_target_pairs={{0,24},{8,0},{16,8},{24,16},{1,25},{9,1},{17,9},{25,17},{2,26},{10... | collective-permute-start | bytes 34568 | tf_op jit(solution)/shard_map/ppermute | solution.py:20
  72.6 14.4 %copy-start.38 = (f32[4,15,35,1]{2,1,0,3:T(8,128)S(1)}, f32[4,15,35,1]{2,1,0,3:T(8,128)}, u32[]{:S(2)}) copy-start(f32[4,15,35,1]{2,1,0,3:T(8,128)} %constant.47) | copy-start | bytes 25204
  82.7 4.2 collective-permute-start.1
  114.3 11.9 %all-to-all-start.5 = ((f32[8,1,360]{2,1,0:T(1,128)}), f32[8,1,360]{2,1,0:T(1,128)}, u32[]{:S(2)}, u32[]{:S(2)}) async-start(f32[8,1,360]{2,1,0:T(1,128)} %reshape.533), calls=%async_computation.5 | async-start | bytes 24576 | tf_op jit(solution)/shard_map/all_to_all | solution.py:62
  126.1 8.9 %all-to-all-start.4 = ((f32[8,1,360]{2,1,0:T(1,128)}), f32[8,1,360]{2,1,0:T(1,128)}, u32[]{:S(2)}, u32[]{:S(2)}) async-start(f32[8,1,360]{2,1,0:T(1,128)} %reshape.535), calls=%async_computation.4 | async-start | bytes 24576 | tf_op jit(solution)/shard_map/all_to_all | solution.py:62
  135.1 22.5 %all-to-all-start.3 = ((f32[8,1,360]{2,1,0:T(1,128)}), f32[8,1,360]{2,1,0:T(1,128)}, u32[]{:S(2)}, u32[]{:S(2)}) async-start(f32[8,1,360]{2,1,0:T(1,128)} %reshape.537), calls=%async_computation.3 | async-start | bytes 24576 | tf_op jit(solution)/shard_map/all_to_all | solution.py:62
  152.9 22.8 %collective-permute-start.9 = (f32[3,15,64]{1,0,2:T(4,128)}, f32[3,15,64]{1,0,2:T(4,128)}, u32[]{:S(2)}, u32[]{:S(2)}) collective-permute-start(f32[3,15,64]{1,0,2:T(4,128)} %bitcast.574), channel_id=1, source_target_pairs={{0,8},{8,16},{16,24},{24,0},{1,9},{9,17},{17,25},{25,1},{2,10},{10... | collective-permute-start | bytes 34568 | tf_op jit(solution)/shard_map/ppermute | solution.py:20
  157.1 18.6 %collective-permute-start.8 = (f32[3,15,64]{1,0,2:T(4,128)}, f32[3,15,64]{1,0,2:T(4,128)}, u32[]{:S(2)}, u32[]{:S(2)}) collective-permute-start(f32[3,15,64]{1,0,2:T(4,128)} %bitcast.577), channel_id=1, source_target_pairs={{0,16},{8,24},{16,0},{24,8},{1,17},{9,25},{17,1},{25,9},{2,18},{10... | collective-permute-start | bytes 34568 | tf_op jit(solution)/shard_map/ppermute | solution.py:20
  161.0 14.7 %collective-permute-start.7 = (f32[3,15,64]{1,0,2:T(4,128)}, f32[3,15,64]{1,0,2:T(4,128)}, u32[]{:S(2)}, u32[]{:S(2)}) collective-permute-start(f32[3,15,64]{1,0,2:T(4,128)} %bitcast.580), channel_id=1, source_target_pairs={{0,24},{8,0},{16,8},{24,16},{1,25},{9,1},{17,9},{25,17},{2,26},{10... | collective-permute-start | bytes 34568 | tf_op jit(solution)/shard_map/ppermute | solution.py:20
  173.6 7.5 %collective-permute-start.5 = (f32[3,15,128]{2,1,0:T(8,128)}, f32[3,15,128]{2,1,0:T(8,128)}, u32[]{:S(2)}, u32[]{:S(2)}) collective-permute-start(f32[3,15,128]{2,1,0:T(8,128)} %slice.244), channel_id=1, source_target_pairs={{0,7},{1,0},{2,1},{3,2},{4,3},{5,4},{6,5},{7,6},{8,15},{9,8},{10,9... | collective-permute-start | bytes 69128 | tf_op jit(solution)/shard_map/ppermute | solution.py:20
  179.4 10.7 %copy-start.22 = (f32[3,35,1024]{2,1,0:T(8,128)S(1)}, f32[3,35,1024]{2,1,0:T(8,128)}, u32[]{:S(2)}) copy-start(f32[3,35,1024]{2,1,0:T(8,128)} %get-tuple-element.28) | copy-start | bytes 1290244
  179.4 10.7 %copy-start.57 = (f32[1024]{0:T(1024)S(1)}, f32[1024]{0:T(1024)}, u32[]{:S(2)}) copy-start(f32[1024]{0:T(1024)} %param.17) | copy-start | bytes 12292
  183.6 4.6 %collective-permute-start.6 = (f32[3,15,128]{2,1,0:T(8,128)S(1)}, f32[3,15,128]{2,1,0:T(8,128)S(1)}, u32[]{:S(2)}, u32[]{:S(2)}) collective-permute-start(f32[3,15,128]{2,1,0:T(8,128)S(1)} %fusion.86), channel_id=1, source_target_pairs={{0,1},{1,2},{2,3},{3,4},{4,5},{5,6},{6,7},{7,0},{8,9},{9,10},{10,1... | collective-permute-start | bytes 69128 | tf_op jit(solution)/shard_map/ppermute | solution.py:20
  212.1 9.8 %all-to-all-start.8 = ((f32[8,1,360]{2,1,0:T(1,128)}), f32[8,1,360]{2,1,0:T(1,128)S(1)}, u32[]{:S(2)}, u32[]{:S(2)}) async-start(f32[8,1,360]{2,1,0:T(1,128)} %reshape.539), calls=%async_computation.8 | async-start | bytes 24576 | tf_op jit(solution)/shard_map/all_to_all | solution.py:62
  221.9 8.9 %all-to-all-start.7 = ((f32[8,1,360]{2,1,0:T(1,128)}), f32[8,1,360]{2,1,0:T(1,128)S(1)}, u32[]{:S(2)}, u32[]{:S(2)}) async-start(f32[8,1,360]{2,1,0:T(1,128)} %reshape.541), calls=%async_computation.7 | async-start | bytes 24576 | tf_op jit(solution)/shard_map/all_to_all | solution.py:62
  230.8 20.6 %all-to-all-start.6 = ((f32[8,1,360]{2,1,0:T(1,128)}), f32[8,1,360]{2,1,0:T(1,128)}, u32[]{:S(2)}, u32[]{:S(2)}) async-start(f32[8,1,360]{2,1,0:T(1,128)} %reshape.543), calls=%async_computation.6 | async-start | bytes 24576 | tf_op jit(solution)/shard_map/all_to_all | solution.py:62
  239.4 17.3 %copy-start.33 = (f32[3,3072]{1,0:T(4,128)S(1)}, f32[3,3072]{1,0:T(4,128)}, u32[]{:S(2)}) copy-start(f32[3,3072]{1,0:T(4,128)} %get-tuple-element.20) | copy-start | bytes 110596
  239.4 17.3 %copy-start.48 = (f32[1,3072]{1,0:T(1,128)S(1)}, f32[1,3072]{1,0:T(1,128)}, u32[]{:S(2)}) copy-start(f32[1,3072]{1,0:T(1,128)} %copy-done.47) | copy-start | bytes 36868
  239.4 17.3 %copy-start.52 = (pred[3072]{0:T(1024)(128)(4,1)S(1)}, pred[3072]{0:T(1024)(128)(4,1)}, u32[]{:S(2)}) copy-start(pred[3072]{0:T(1024)(128)(4,1)} %get-tuple-element.2) | copy-start | bytes 9220
  239.4 17.3 %copy-start.55 = (pred[3072]{0:T(1024)(128)(4,1)S(1)}, pred[3072]{0:T(1024)(128)(4,1)}, u32[]{:S(2)}) copy-start(pred[3072]{0:T(1024)(128)(4,1)} %get-tuple-element.3) | copy-start | bytes 9220
  247.5 21.8 %collective-permute-start.14 = (f32[3,15,64]{1,0,2:T(4,128)}, f32[3,15,64]{1,0,2:T(4,128)}, u32[]{:S(2)}, u32[]{:S(2)}) collective-permute-start(f32[3,15,64]{1,0,2:T(4,128)} %bitcast.575), channel_id=1, source_target_pairs={{0,8},{8,16},{16,24},{24,0},{1,9},{9,17},{17,25},{25,1},{2,10},{10... | collective-permute-start | bytes 34568 | tf_op jit(solution)/shard_map/ppermute | solution.py:20
  250.2 19.1 %collective-permute-start.13 = (f32[3,15,64]{1,0,2:T(4,128)}, f32[3,15,64]{1,0,2:T(4,128)}, u32[]{:S(2)}, u32[]{:S(2)}) collective-permute-start(f32[3,15,64]{1,0,2:T(4,128)} %bitcast.578), channel_id=1, source_target_pairs={{0,16},{8,24},{16,0},{24,8},{1,17},{9,25},{17,1},{25,9},{2,18},{10... | collective-permute-start | bytes 34568 | tf_op jit(solution)/shard_map/ppermute | solution.py:20
  253.6 15.7 %collective-permute-start.12 = (f32[3,15,64]{1,0,2:T(4,128)}, f32[3,15,64]{1,0,2:T(4,128)}, u32[]{:S(2)}, u32[]{:S(2)}) collective-permute-start(f32[3,15,64]{1,0,2:T(4,128)} %bitcast.581), channel_id=1, source_target_pairs={{0,24},{8,0},{16,8},{24,16},{1,25},{9,1},{17,9},{25,17},{2,26},{10... | collective-permute-start | bytes 34568 | tf_op jit(solution)/shard_map/ppermute | solution.py:20
  262.9 17.9 %copy-start.39 = (f32[4,15,35,1]{2,1,0,3:T(8,128)S(1)}, f32[4,15,35,1]{2,1,0,3:T(8,128)}, u32[]{:S(2)}) copy-start(f32[4,15,35,1]{2,1,0,3:T(8,128)} %constant.47) | copy-start | bytes 25204
  267.6 6.5 %collective-permute-start.10 = (f32[3,15,128]{2,1,0:T(8,128)}, f32[3,15,128]{2,1,0:T(8,128)}, u32[]{:S(2)}, u32[]{:S(2)}) collective-permute-start(f32[3,15,128]{2,1,0:T(8,128)} %slice.252), channel_id=1, source_target_pairs={{0,7},{1,0},{2,1},{3,2},{4,3},{5,4},{6,5},{7,6},{8,15},{9,8},{10,9... | collective-permute-start | bytes 69128 | tf_op jit(solution)/shard_map/ppermute | solution.py:20
  276.6 4.2 collective-permute-start.11
  308.4 11.9 %all-to-all-start.11 = ((f32[8,1,360]{2,1,0:T(1,128)}), f32[8,1,360]{2,1,0:T(1,128)}, u32[]{:S(2)}, u32[]{:S(2)}) async-start(f32[8,1,360]{2,1,0:T(1,128)} %reshape.545), calls=%async_computation.11 | async-start | bytes 24576 | tf_op jit(solution)/shard_map/all_to_all | solution.py:62
  320.3 8.9 %all-to-all-start.10 = ((f32[8,1,360]{2,1,0:T(1,128)}), f32[8,1,360]{2,1,0:T(1,128)}, u32[]{:S(2)}, u32[]{:S(2)}) async-start(f32[8,1,360]{2,1,0:T(1,128)} %reshape.547), calls=%async_computation.10 | async-start | bytes 24576 | tf_op jit(solution)/shard_map/all_to_all | solution.py:62
  329.3 22.5 %all-to-all-start.9 = ((f32[8,1,360]{2,1,0:T(1,128)}), f32[8,1,360]{2,1,0:T(1,128)}, u32[]{:S(2)}, u32[]{:S(2)}) async-start(f32[8,1,360]{2,1,0:T(1,128)} %reshape.549), calls=%async_computation.9 | async-start | bytes 24576 | tf_op jit(solution)/shard_map/all_to_all | solution.py:62
  347.1 22.8 %collective-permute-start.19 = (f32[3,15,64]{1,0,2:T(4,128)}, f32[3,15,64]{1,0,2:T(4,128)}, u32[]{:S(2)}, u32[]{:S(2)}) collective-permute-start(f32[3,15,64]{1,0,2:T(4,128)} %bitcast.576), channel_id=1, source_target_pairs={{0,8},{8,16},{16,24},{24,0},{1,9},{9,17},{17,25},{25,1},{2,10},{10... | collective-permute-start | bytes 34568 | tf_op jit(solution)/shard_map/ppermute | solution.py:20
  350.6 19.3 %collective-permute-start.18 = (f32[3,15,64]{1,0,2:T(4,128)}, f32[3,15,64]{1,0,2:T(4,128)}, u32[]{:S(2)}, u32[]{:S(2)}) collective-permute-start(f32[3,15,64]{1,0,2:T(4,128)} %bitcast.579), channel_id=1, source_target_pairs={{0,16},{8,24},{16,0},{24,8},{1,17},{9,25},{17,1},{25,9},{2,18},{10... | collective-permute-start | bytes 34568 | tf_op jit(solution)/shard_map/ppermute | solution.py:20
  355.2 14.7 %collective-permute-start.17 = (f32[3,15,64]{1,0,2:T(4,128)}, f32[3,15,64]{1,0,2:T(4,128)}, u32[]{:S(2)}, u32[]{:S(2)}) collective-permute-start(f32[3,15,64]{1,0,2:T(4,128)} %bitcast.582), channel_id=1, source_target_pairs={{0,24},{8,0},{16,8},{24,16},{1,25},{9,1},{17,9},{25,17},{2,26},{10... | collective-permute-start | bytes 34568 | tf_op jit(solution)/shard_map/ppermute | solution.py:20
  368.1 7.2 %collective-permute-start.15 = (f32[3,15,128]{2,1,0:T(8,128)}, f32[3,15,128]{2,1,0:T(8,128)}, u32[]{:S(2)}, u32[]{:S(2)}) collective-permute-start(f32[3,15,128]{2,1,0:T(8,128)} %slice.260), channel_id=1, source_target_pairs={{0,7},{1,0},{2,1},{3,2},{4,3},{5,4},{6,5},{7,6},{8,15},{9,8},{10,9... | collective-permute-start | bytes 69128 | tf_op jit(solution)/shard_map/ppermute | solution.py:20
  373.5 10.5 %copy-start.21 = (f32[3,35,1024]{2,1,0:T(8,128)S(1)}, f32[3,35,1024]{2,1,0:T(8,128)}, u32[]{:S(2)}) copy-start(f32[3,35,1024]{2,1,0:T(8,128)} %get-tuple-element.36) | copy-start | bytes 1290244
  373.5 10.5 %copy-start.58 = (f32[1024]{0:T(1024)S(1)}, f32[1024]{0:T(1024)}, u32[]{:S(2)}) copy-start(f32[1024]{0:T(1024)} %param.17) | copy-start | bytes 12292
  377.8 4.4 collective-permute-start.16
  406.0 9.8 %all-to-all-start.14 = ((f32[8,1,360]{2,1,0:T(1,128)}), f32[8,1,360]{2,1,0:T(1,128)S(1)}, u32[]{:S(2)}, u32[]{:S(2)}) async-start(f32[8,1,360]{2,1,0:T(1,128)} %reshape.551), calls=%async_computation.14 | async-start | bytes 24576 | tf_op jit(solution)/shard_map/all_to_all | solution.py:62
  415.8 8.9 %all-to-all-start.13 = ((f32[8,1,360]{2,1,0:T(1,128)}), f32[8,1,360]{2,1,0:T(1,128)S(1)}, u32[]{:S(2)}, u32[]{:S(2)}) async-start(f32[8,1,360]{2,1,0:T(1,128)} %reshape.553), calls=%async_computation.13 | async-start | bytes 24576 | tf_op jit(solution)/shard_map/all_to_all | solution.py:62
  424.7 13.9 %all-to-all-start.12 = ((f32[8,1,360]{2,1,0:T(1,128)}), f32[8,1,360]{2,1,0:T(1,128)S(1)}, u32[]{:S(2)}, u32[]{:S(2)}) async-start(f32[8,1,360]{2,1,0:T(1,128)} %reshape.555), calls=%async_computation.12 | async-start | bytes 24576 | tf_op jit(solution)/shard_map/all_to_all | solution.py:62
  432.7 10.5 %copy-start.31 = (f32[2,8,24,128]{3,1,2,0:T(8,128)S(1)}, f32[2,8,24,128]{3,1,2,0:T(8,128)}, u32[]{:S(2)}) copy-start(f32[2,8,24,128]{3,1,2,0:T(8,128)} %copy.503) | copy-start | bytes 589828
  432.7 10.5 %copy-start.34 = (f32[3,3072]{1,0:T(4,128)S(1)}, f32[3,3072]{1,0:T(4,128)}, u32[]{:S(2)}) copy-start(f32[3,3072]{1,0:T(4,128)} %get-tuple-element.20) | copy-start | bytes 110596
  432.7 10.5 %copy-start.49 = (f32[1,3072]{1,0:T(1,128)S(1)}, f32[1,3072]{1,0:T(1,128)}, u32[]{:S(2)}) copy-start(f32[1,3072]{1,0:T(1,128)} %copy-done.47) | copy-start | bytes 36868
  432.7 10.5 %copy-start.53 = (pred[3072]{0:T(1024)(128)(4,1)S(1)}, pred[3072]{0:T(1024)(128)(4,1)}, u32[]{:S(2)}) copy-start(pred[3072]{0:T(1024)(128)(4,1)} %get-tuple-element.2) | copy-start | bytes 9220
  435.3 15.0 %collective-permute-start.24 = (f32[3,15,64]{1,0,2:T(4,128)}, f32[3,15,64]{1,0,2:T(4,128)}, u32[]{:S(2)}, u32[]{:S(2)}) collective-permute-start(f32[3,15,64]{1,0,2:T(4,128)} %bitcast.420), channel_id=1, source_target_pairs={{0,8},{8,16},{16,24},{24,0},{1,9},{9,17},{17,25},{25,1},{2,10},{10... | collective-permute-start | bytes 34568 | tf_op jit(solution)/shard_map/ppermute | solution.py:20
  437.4 12.9 %collective-permute-start.23 = (f32[3,15,64]{1,0,2:T(4,128)}, f32[3,15,64]{1,0,2:T(4,128)}, u32[]{:S(2)}, u32[]{:S(2)}) collective-permute-start(f32[3,15,64]{1,0,2:T(4,128)} %bitcast.422), channel_id=1, source_target_pairs={{0,16},{8,24},{16,0},{24,8},{1,17},{9,25},{17,1},{25,9},{2,18},{10... | collective-permute-start | bytes 34568 | tf_op jit(solution)/shard_map/ppermute | solution.py:20
  440.1 10.3 %collective-permute-start.22 = (f32[3,15,64]{1,0,2:T(4,128)}, f32[3,15,64]{1,0,2:T(4,128)}, u32[]{:S(2)}, u32[]{:S(2)}) collective-permute-start(f32[3,15,64]{1,0,2:T(4,128)} %bitcast.424), channel_id=1, source_target_pairs={{0,24},{8,0},{16,8},{24,16},{1,25},{9,1},{17,9},{25,17},{2,26},{10... | collective-permute-start | bytes 34568 | tf_op jit(solution)/shard_map/ppermute | solution.py:20
  448.5 3.3 collective-permute-start.20
  452.1 4.2 collective-permute-start.21
  (59 other events, 283.4 us)
where the time goes:
time: 468 us; the launch traced here: 459 us
  local copies, waits for them, and re-layouts  174 us (37%)
  starting transfers between devices  103 us (22%)
  matrix products  99.3 us (21%)
  other arithmetic  53.7 us (11%)
  waiting for transfers between devices  25.8 us (6%)
    unnamed x228, local copies, waits for them, and re-layouts  64.8 us
    all_to_all x15, starting transfers between devices, route_traces(): lax.all_to_all(blocks[:, :, offset], 'sub', split_axis=2, concat_axis=2,...  57.8 us
    ppermute x25, starting transfers between devices, shifted(): return lax.ppermute(value, axis, pairs)  45.4 us
    dot_general x5, matrix products, shards(): jnp.dot(strain_map.T, weighted, precision=highest)  22.4 us
    dot_general x15, matrix products, apply_mass(): spread = jnp.einsum('ij,cjf->cif', face_mass, traction, precision=highest)  20 us
    all_to_all x15, other arithmetic, route_traces(): lax.all_to_all(blocks[:, :, offset], 'sub', split_axis=2, concat_axis=2,...  19.9 us
    dot_general x5, matrix products, shards(): jnp.dot(strain_map, field.reshape(components * node_count, elements), pre...  18.2 us
    ppermute x25, waiting for transfers between devices, shifted(): return lax.ppermute(value, axis, pairs)  16.2 us
  transfers between devices with their start and end apart: 40, of which 11 were waited for; matrix products, arithmetic and copies ran while one was open for 45% of the time, Pallas kernels for 0%

commit v1 on v0

v1 whole, which is shorter than its diff:
```python
import functools
import math

import jax
import jax.numpy as jnp
import numpy as np
from jax import lax
from jax.experimental import pallas as pl
from jax.experimental.pallas import tpu as pltpu
from jax.sharding import PartitionSpec as P

BLOCK = 128
PAD = 40
ROWS = 128
FACE = 16
TRACE = 3 * FACE
TILE = 256

shear_weight = 0.5
opening_scale = 4.0
time_step = 0.25
highest = lax.Precision.HIGHEST
bf16 = jnp.bfloat16
f32 = jnp.float32


def face_table():
    points = [
        (first, second, third, 4 - first - second - third)
        for first in range(5)
        for second in range(5 - first)
        for third in range(5 - first - second)
    ]
    result = np.zeros((4, 15, 35), np.float32)
    for side in range(4):
        members = [index for index, point in enumerate(points) if point[side] == 0]
        for place, index in enumerate(members):
            result[side, place, index] = 1.0
    return result


def tables():
    table = face_table()
    nodes = table.shape[2]
    spread = np.zeros((3 * nodes, ROWS), np.float32)
    rows = np.zeros((ROWS, nodes), np.float32)
    for c in range(3):
        for n in range(nodes):
            spread[c * nodes + n, c * PAD + n] = 1.0
            rows[c * PAD + n, n] = 1.0
    place = np.zeros((3 * TRACE, 15), np.float32)
    lift = np.zeros((ROWS, 3 * TRACE), np.float32)
    lift0 = np.zeros((ROWS, TRACE), np.float32)
    for c in range(3):
        for i in range(15):
            for k in range(3):
                place[k * TRACE + c * FACE + i, i] = 1.0
                for n in range(nodes):
                    lift[c * PAD + n, k * TRACE + c * FACE + i] = table[k + 1, i, n]
            for n in range(nodes):
                lift0[c * PAD + n, c * FACE + i] = table[0, i, n]
    pick = np.concatenate([lift.T, lift.T], axis=1)
    return spread, rows, place, lift, lift0, pick


def dot(a, b):
    return lax.dot_general(a, b, (((1,), (0,)), ((), ())), preferred_element_type=f32)


def dot_full(a, b):
    return lax.dot_general(
        a, b, (((1,), (0,)), ((), ())), precision=highest, preferred_element_type=f32
    )


def dot_full_t(a, b):
    return lax.dot_general(
        a, b, (((1,), (1,)), ((), ())), precision=highest, preferred_element_type=f32
    )


def pieces(value):
    high = value.astype(bf16)
    low = (value - high.astype(f32)).astype(bf16)
    return high, low


def traction(jump, normal, weight0, weight1):
    j0, j1, j2 = jump
    n0, n1, n2 = normal
    along = n0 * j0 + n1 * j1 + n2 * j2
    t0, t1, t2 = j0 - along * n0, j1 - along * n1, j2 - along * n2
    opening = along * along + shear_weight * (t0 * t0 + t1 * t1 + t2 * t2)
    beta = weight1 * jnp.exp(opening * (-1.0 / opening_scale))
    alpha = weight0 + beta
    gamma = beta * along
    return [alpha * j0 + gamma * n0, alpha * j1 + gamma * n1, alpha * j2 + gamma * n2]


def build_inner(links, geometry, weights, jac, coef, index):
    inverse = 1.0 / jac
    for q in range(3):
        geo = geometry(q)
        link = links(q)
        partner = link[0:1, :]
        state = link[1:2, :]
        scale = geo[3:4, :] * inverse
        coef[5 * q : 5 * q + 3, :] = geo[0:3, :]
        coef[5 * q + 3 : 5 * q + 4, :] = jnp.where(state == 0, scale, 0.0)
        coef[5 * q + 4 : 5 * q + 5, :] = jnp.where(state == 1, (1.0 - shear_weight) * scale, 0.0)
        index[q : q + 1, :] = lax.bitwise_and(partner, BLOCK - 1)
        index[3 + q : 4 + q, :] = lax.div(partner, BLOCK)
    count = weights.shape[0]
    coef[15 : 15 + count, :] = weights * inverse


def local_change(field, at, coef, index, ops):
    high_op, low_op, pick, lift = ops
    lanes = pl.ds(at, TILE)
    high, low = pieces(field[:, lanes])
    both = jnp.concatenate([high, low], axis=0)
    total = None
    for m in range(high_op.shape[0]):
        part = dot(high_op[m], both) + dot(low_op[m], both)
        part = part * coef[15 + m : 16 + m, lanes]
        total = part if total is None else total + part
    traces = dot(pick[...], both)
    halves = []
    for half in range(TILE // BLOCK):
        start = at + half * BLOCK
        part = traces[:, half * BLOCK : (half + 1) * BLOCK]
        forces = []
        for q in range(3):
            where = jnp.broadcast_to(index[q : q + 1, pl.ds(start, BLOCK)], (TRACE, BLOCK))
            side = index[3 + q : 4 + q, pl.ds(start, BLOCK)]
            found = [
                jnp.take_along_axis(
                    part[k * TRACE : (k + 1) * TRACE], where, axis=1, mode="promise_in_bounds"
                )
                for k in range(3)
            ]
            paired = jnp.where(side == 0, found[0], jnp.where(side == 1, found[1], found[2]))
            jump = paired - part[q * TRACE : (q + 1) * TRACE]
            rows = [coef[5 * q + r : 5 * q + r + 1, pl.ds(start, BLOCK)] for r in range(5)]
            forces += traction(
                [jump[c * FACE : (c + 1) * FACE] for c in range(3)], rows[0:3], rows[3], rows[4]
            )
        halves.append(jnp.concatenate(forces, axis=0))
    high, low = pieces(jnp.concatenate(halves, axis=1))
    first = dot(lift[...], high)
    second = dot(lift[0:ROWS, :], low)
    return total + (first[0:ROWS] + first[ROWS : 2 * ROWS] + second)


def load_state(source, target):
    target[...] = jnp.zeros_like(target)
    for c in range(3):
        target[c * PAD : c * PAD + source.shape[1], :] = source[c]


def trace_of(field, lanes):
    return [field[c * PAD : c * PAD + FACE, lanes] for c in range(3)]


def pack(first, second, extra, shared, groups, places, upper, lower, cross):
    parts = [first]
    if second is not None:
        parts.append(second)
    if extra is not None:
        parts.append(extra)
    rows = jnp.concatenate(parts, axis=0)
    upper[...] = rows[:, 0:shared]
    lower[...] = rows[:, shared : 2 * shared]
    rest = rows[:, 2 * shared :]
    missing = BLOCK - rest.shape[0]
    rest = jnp.concatenate([rest, jnp.zeros((missing, rest.shape[1]), f32)], axis=0)
    blocks = rest.T.reshape(rest.shape[1] // 8, 8, BLOCK)
    group = lax.axis_index("group")
    cross[pl.ds(group * places, places)] = jnp.zeros((places, 8, BLOCK), f32)
    for b in range(groups - 1):
        target = lax.rem(group + (1 + b), groups)
        cross[pl.ds(target * places, places)] = blocks[b * places : (b + 1) * places]


def unpack(upper, lower, cross, groups, places, width):
    group = lax.axis_index("group")
    parts = []
    for b in range(groups - 1):
        source = lax.rem(group + (1 + b), groups)
        parts.append(cross[pl.ds(source * places, places)].reshape(places * 8, BLOCK))
    spare = width - (groups - 1) * places * 8
    if spare:
        parts.append(jnp.zeros((spare, BLOCK), f32))
    slots = jnp.concatenate(parts, axis=0).T
    return jnp.concatenate([upper[...], lower[...], slots[0 : upper.shape[0]]], axis=1)


def split_rows(value):
    return [value[c * FACE : (c + 1) * FACE] for c in range(3)]


def rim_traction(jump, rim):
    rows = [rim[r : r + 1, :] for r in range(5)]
    return jnp.concatenate(traction(split_rows(jump), rows[0:3], rows[3], rows[4]), axis=0)


def times_lift0(lift0, value):
    high, low = pieces(value)
    return dot(lift0[...], jnp.concatenate([high, low, high], axis=0))


def first_pack(sizes, disp, jac, upper, lower, cross):
    shared, groups, places, rim_lanes = sizes
    trace = jnp.concatenate([disp[c, 0:FACE, :] for c in range(3)], axis=0)
    extra = jnp.broadcast_to(1.0 / jac[:, 0:rim_lanes], (8, rim_lanes))
    pack(trace, None, extra, shared, groups, places, upper, lower, cross)


def prepare(
    sizes,
    strain,
    face_mass,
    mass_inverse,
    spread,
    rows,
    place,
    lift,
    lift0,
    high_op,
    low_op,
    lift_op,
    lift0_op,
    trace_op,
):
    size = strain.shape[1]
    row = lax.broadcasted_iota(jnp.int32, (ROWS, ROWS), 0)
    col = lax.broadcasted_iota(jnp.int32, (ROWS, ROWS), 1)
    inverse = dot_full_t(dot_full(rows[...], mass_inverse[...]), rows[...])
    inverse = jnp.where(lax.div(row, PAD) == lax.div(col, PAD), inverse, 0.0)
    inverse = inverse * (time_step * time_step)
    for m in range(high_op.shape[0]):
        block = dot_full(strain[m * size : (m + 1) * size, :], spread[...])
        value = -dot_full(dot_full_t(inverse, block), block)
        high, low = pieces(value)
        high_op[m] = jnp.concatenate([high, high], axis=1)
        low_op[m] = jnp.concatenate([low, low], axis=1)
    wide = 3 * TRACE
    row = lax.broadcasted_iota(jnp.int32, (wide, wide), 0)
    col = lax.broadcasted_iota(jnp.int32, (wide, wide), 1)
    mass = dot_full_t(dot_full(place[...], face_mass[...]), place[...])
    same = lax.rem(lax.div(row, FACE), 3) == lax.rem(lax.div(col, FACE), 3)
    mass = jnp.where(same, mass, 0.0)
    inner = jnp.where(lax.div(row, TRACE) == lax.div(col, TRACE), mass, 0.0)
    value = dot_full(inverse, dot_full(lift[...], inner))
    high, low = pieces(value)
    lift_op[0:ROWS, :] = high
    lift_op[ROWS : 2 * ROWS, :] = low
    value = dot_full(inverse, dot_full(lift0[...], mass[0:TRACE, :]))

    def three(value):
        high = value.astype(bf16).astype(f32)
        col = lax.broadcasted_iota(jnp.int32, value.shape, 1)
        return jnp.where(col < 2 * TRACE, high, value - high).astype(bf16)

    lift0_op[...] = three(value)
    trace_op[...] = three(
        jnp.concatenate([value[c * PAD : c * PAD + FACE] for c in range(3)], axis=0)
    )


def start_rim(
    sizes,
    disp,
    vel,
    links,
    geometry,
    weights,
    jac,
    next_links,
    next_geometry,
    cross_links,
    cross_geometry,
    high_op,
    low_op,
    pick,
    lift_op,
    field_out,
    vel_out,
    coef,
    index,
    rim,
):
    shared, groups, places, lanes = sizes
    elements = links.shape[1] // 3
    inverse = jac[:, 0:lanes]
    build_inner(
        lambda q: links[:, q * elements : q * elements + lanes],
        lambda q: geometry[:, q * elements : q * elements + lanes],
        weights[:, 0:lanes],
        inverse,
        coef,
        index,
    )
    rim[...] = jnp.zeros_like(rim)
    slots = cross_links.shape[1]
    for at, count, geo, state in (
        (0, shared, next_geometry[0:4, :], next_links[0:1, :]),
        (shared, shared, next_geometry[4:8, :], next_links[1:2, :]),
        (2 * shared, slots, cross_geometry[...], cross_links[...]),
    ):
        rim[0:3, at : at + count] = geo[0:3, :]
        rim[3:4, at : at + count] = jnp.where(state == 0, 1.0, 0.0)
        rim[4:5, at : at + count] = jnp.where(state == 1, 1.0 - shear_weight, 0.0)
        rim[6:7, at : at + count] = geo[3:4, :]
    rim[5:6, :] = rim[6:7, :] * (1.0 / inverse)
    load_state(disp, field_out)
    load_state(vel, vel_out)
    ops = (high_op, low_op, pick, lift_op)
    for at in range(0, lanes, TILE):
        span = pl.ds(at, TILE)
        vel_out[:, span] = time_step * vel_out[:, span] + local_change(
            field_out, at, coef, index, ops
        )


def first_step(
    sizes,
    upper_in,
    lower_in,
    cross_in,
    field,
    vel,
    coef,
    index,
    rim,
    high_op,
    low_op,
    pick,
    lift_op,
    lift0_op,
    field_out,
    vel_out,
    own_out,
    rim_out,
    upper,
    lower,
    cross,
):
    shared, groups, places, lanes = sizes
    every = slice(None)
    arrived = unpack(upper_in, lower_in, cross_in, groups, places, lanes - 2 * shared)
    own = jnp.concatenate(trace_of(field, every), axis=0)
    pull = rim_traction(arrived[0:TRACE] - own, rim)
    rim_out[0:6, :] = rim[0:6, :]
    rim_out[6:7, :] = rim[5:6, :] + rim[6:7, :] * arrived[TRACE : TRACE + 1]
    rim_out[7:8, :] = rim[7:8, :]
    change = times_lift0(lift0_op, pull * rim[5:6, :])
    speed = vel[...] + change
    vel_out[...] = speed
    field_out[...] = field[...] + speed
    send_two(sizes, field_out, vel_out, own_out, coef, index, (high_op, low_op, pick, lift_op), upper, lower, cross)


def send_two(sizes, field_out, vel_out, own_out, coef, index, ops, upper, lower, cross):
    shared, groups, places, lanes = sizes
    every = slice(None)
    first = jnp.concatenate(trace_of(field_out, every), axis=0)
    own_out[...] = first
    for at in range(0, lanes, TILE):
        span = pl.ds(at, TILE)
        speed = vel_out[:, span] + local_change(field_out, at, coef, index, ops)
        vel_out[:, span] = speed
        field_out[:, span] = field_out[:, span] + speed
    second = jnp.concatenate(trace_of(field_out, every), axis=0)
    pack(first, second, None, shared, groups, places, upper, lower, cross)


def take_two(sizes, upper_in, lower_in, cross_in, field, vel, own, coef, index, rim, ops, lift0_op, trace_op, field_out, vel_out):
    shared, groups, places, lanes = sizes
    every = slice(None)
    arrived = unpack(upper_in, lower_in, cross_in, groups, places, lanes - 2 * shared)
    pull = rim_traction(arrived[0:TRACE] - own[...], rim)
    later = arrived[TRACE : 2 * TRACE] - jnp.concatenate(trace_of(field, every), axis=0)
    later = later - times_lift0(trace_op, pull * rim[6:7, :])
    pull_later = rim_traction(later, rim)
    change = times_lift0(lift0_op, pull * rim[5:6, :])
    vel_out[...] = vel[...] + change
    field_out[...] = field[...] + change
    change = times_lift0(lift0_op, pull_later * rim[5:6, :])
    for at in range(0, lanes, TILE):
        span = pl.ds(at, TILE)
        speed = vel_out[:, span] + (
            local_change(field_out, at, coef, index, ops) + change[:, at : at + TILE]
        )
        vel_out[:, span] = speed
        field_out[:, span] = field_out[:, span] + speed


def middle_steps(
    sizes,
    upper_in,
    lower_in,
    cross_in,
    field,
    vel,
    own,
    coef,
    index,
    rim,
    high_op,
    low_op,
    pick,
    lift_op,
    lift0_op,
    trace_op,
    field_out,
    vel_out,
    own_out,
    upper,
    lower,
    cross,
):
    ops = (high_op, low_op, pick, lift_op)
    take_two(sizes, upper_in, lower_in, cross_in, field, vel, own, coef, index, rim, ops, lift0_op, trace_op, field_out, vel_out)
    send_two(sizes, field_out, vel_out, own_out, coef, index, ops, upper, lower, cross)


def last_steps(
    sizes,
    upper_in,
    lower_in,
    cross_in,
    field,
    vel,
    own,
    coef,
    index,
    rim,
    high_op,
    low_op,
    pick,
    lift_op,
    lift0_op,
    trace_op,
    *rest,
):
    disp_out, vel_out, field_new, vel_new = rest[-4:]
    ops = (high_op, low_op, pick, lift_op)
    take_two(sizes, upper_in, lower_in, cross_in, field, vel, own, coef, index, rim, ops, lift0_op, trace_op, field_new, vel_new)
    store_state(field_new, vel_new, disp_out, vel_out)


def store_state(field, vel, disp_out, vel_out):
    for c in range(3):
        nodes = disp_out.shape[1]
        disp_out[c] = field[c * PAD : c * PAD + nodes, :]
        vel_out[c] = (1.0 / time_step) * vel[c * PAD : c * PAD + nodes, :]


def inside(
    steps,
    disp,
    vel,
    link1,
    link2,
    link3,
    geo1,
    geo2,
    geo3,
    weights,
    jac,
    high_op,
    low_op,
    pick,
    lift_op,
    disp_out,
    vel_out,
    field,
    speed,
    coef,
    index,
):
    links = (link1, link2, link3)
    geos = (geo1, geo2, geo3)
    build_inner(
        lambda q: links[q][...], lambda q: geos[q][...], weights[...], jac[...], coef, index
    )
    load_state(disp, field)
    load_state(vel, speed)
    speed[...] = time_step * speed[...]
    ops = (high_op, low_op, pick, lift_op)

    def step(_, carry):
        for at in range(0, field.shape[1], TILE):
            span = pl.ds(at, TILE)
            new = speed[:, span] + local_change(field, at, coef, index, ops)
            speed[:, span] = new
            field[:, span] = field[:, span] + new
        return carry

    lax.fori_loop(0, steps, step, 0)
    store_state(field, speed, disp_out, vel_out)


def struct(shape, dtype=f32):
    return jax.ShapeDtypeStruct(shape, dtype)


def cost(flops):
    return pl.CostEstimate(flops=flops, bytes_accessed=1 << 20, transcendentals=0)


def shifted(value, axis, steps):
    count = lax.axis_size(axis)
    pairs = [(source, (source + steps) % count) for source in range(count)]
    return lax.ppermute(value, axis, pairs)


def exchange(upper, lower, cross):
    mixed = lax.all_to_all(cross, ("group", "sub"), 0, 0, tiled=True)
    return shifted(lower, "sub", -1), shifted(upper, "sub", 1), mixed


def shards(
    displacement,
    velocity,
    geometry_weights,
    jacobian,
    strain_map,
    face_mass,
    mass_inverse,
    local_links,
    local_geometry,
    neighbour_links,
    neighbour_geometry,
    cross_links,
    cross_geometry,
):
    components, nodes, elements = displacement.shape
    count = geometry_weights.shape[0]
    groups = lax.axis_size("group")
    places = lax.axis_size("sub")
    slots = cross_links.shape[0]
    shared = neighbour_links.shape[1]
    lanes = math.ceil((2 * shared + slots) / TILE) * TILE
    sizes = (shared, groups, places, lanes)
    spread, rows, place, lift, lift0, pick = (jnp.asarray(t) for t in tables())
    pick = pick.astype(bf16)
    jac = jacobian.reshape(1, elements)
    cross_row = cross_links.reshape(1, slots)
    state_shape = struct((ROWS, lanes))
    vmem = pl.BlockSpec(memory_space=pltpu.VMEM)
    part = pl.BlockSpec((components, nodes, lanes), lambda i: (0, 0, 0))
    devices = groups * places

    def messages(height):
        return (struct((height, shared)), struct((height, shared)), struct((devices, 8, BLOCK)))

    sends = pl.pallas_call(
        functools.partial(first_pack, sizes),
        grid=(1,),
        out_shape=messages(TRACE + 8),
        in_specs=[part, vmem],
        cost_estimate=cost(1 << 20),
        name="first_pack",
    )(displacement, jac)
    arrived = exchange(*sends)

    high_op, low_op, lift_op, lift0_op, trace_op = pl.pallas_call(
        functools.partial(prepare, sizes),
        out_shape=(
            struct((count, ROWS, 2 * ROWS), bf16),
            struct((count, ROWS, 2 * ROWS), bf16),
            struct((2 * ROWS, 3 * TRACE), bf16),
            struct((ROWS, 3 * TRACE), bf16),
            struct((TRACE, 3 * TRACE), bf16),
        ),
        cost_estimate=cost(1 << 24),
        name="prepare",
    )(strain_map, face_mass, mass_inverse, spread, rows, place, lift, lift0)

    field, vel, coef, index, rim = pl.pallas_call(
        functools.partial(start_rim, sizes),
        grid=(1,),
        out_shape=(
            state_shape,
            state_shape,
            struct((24, lanes)),
            struct((8, lanes), jnp.int32),
            struct((8, lanes)),
        ),
        in_specs=[part, part] + [vmem] * 12,
        cost_estimate=cost(1 << 24),
        name="start_rim",
    )(
        displacement,
        velocity,
        local_links,
        local_geometry,
        geometry_weights,
        jac,
        neighbour_links,
        neighbour_geometry,
        cross_row,
        cross_geometry,
        high_op,
        low_op,
        pick,
        lift_op,
    )

    field, vel, own, rim, *sends = pl.pallas_call(
        functools.partial(first_step, sizes),
        out_shape=(state_shape, state_shape, struct((TRACE, lanes)), struct((8, lanes)))
        + messages(2 * TRACE),
        cost_estimate=cost(1 << 24),
        name="first_step",
    )(*arrived, field, vel, coef, index, rim, high_op, low_op, pick, lift_op, lift0_op)
    arrived = exchange(*sends)

    inner = elements - lanes
    outputs = []
    if inner:
        width = math.gcd(lanes, inner)
        skip = lanes // width
        per_face = elements // width
        piece = pl.BlockSpec((components, nodes, width), lambda i: (0, 0, skip + i))

        def columns(height, q=0):
            return pl.BlockSpec((height, width), lambda i: (0, q * per_face + skip + i))

        outputs = pl.pallas_call(
            functools.partial(inside, 5),
            grid=(inner // width,),
            out_shape=(struct(displacement.shape), struct(displacement.shape)),
            in_specs=[piece, piece]
            + [columns(2, q) for q in range(3)]
            + [columns(4, q) for q in range(3)]
            + [columns(count), columns(1)]
            + [vmem] * 4,
            out_specs=(piece, piece),
            scratch_shapes=[
                pltpu.VMEM((ROWS, width), f32),
                pltpu.VMEM((ROWS, width), f32),
                pltpu.VMEM((24, width), f32),
                pltpu.VMEM((8, width), jnp.int32),
            ],
            cost_estimate=cost(1 << 26),
            name="inside",
        )(
            displacement,
            velocity,
            *[local_links] * 3,
            *[local_geometry] * 3,
            geometry_weights,
            jac,
            high_op,
            low_op,
            pick,
            lift_op,
        )

    field, vel, own, *sends = pl.pallas_call(
        functools.partial(middle_steps, sizes),
        out_shape=(state_shape, state_shape, struct((TRACE, lanes))) + messages(2 * TRACE),
        cost_estimate=cost(1 << 24),
        name="middle_steps",
    )(*arrived, field, vel, own, coef, index, rim, high_op, low_op, pick, lift_op, lift0_op, trace_op)
    arrived = exchange(*sends)

    anywhere = pl.BlockSpec(memory_space=pl.ANY)
    return pl.pallas_call(
        functools.partial(last_steps, sizes),
        grid=(1,),
        out_shape=(struct(displacement.shape), struct(displacement.shape)),
        in_specs=[vmem] * 15 + [anywhere] * len(outputs),
        out_specs=(part, part),
        scratch_shapes=[pltpu.VMEM((ROWS, lanes), f32), pltpu.VMEM((ROWS, lanes), f32)],
        input_output_aliases={15: 0, 16: 1} if inner else {},
        cost_estimate=cost(1 << 24),
        name="last_steps",
    )(*arrived, field, vel, own, coef, index, rim, high_op, low_op, pick, lift_op, lift0_op, trace_op, *outputs)


def solution(mesh):
    return jax.shard_map(
        shards,
        mesh=mesh,
        in_specs=(
            P(None, None, ("group", "sub")),
            P(None, None, ("group", "sub")),
            P(None, ("group", "sub")),
            P(("group", "sub")),
            P(),
            P(),
            P(),
            P(None, ("group", "sub")),
            P(None, ("group", "sub")),
            P(None, ("group", "sub")),
            P(None, ("group", "sub")),
            P(("group", "sub")),
            P(None, ("group", "sub")),
        ),
        out_specs=(P(None, None, ("group", "sub")), P(None, None, ("group", "sub"))),
        check_vma=False,
    )
```

time: 468 us -> 66.6 us (0.14); the launches traced: 459 us -> 66 us
  local copies, waits for them, and re-layouts: 174 us -> 2.88 us
  matrix products: 99.3 us -> 0 us
  starting transfers between devices: 103 us -> 23.1 us
  other arithmetic: 53.7 us -> 0 us
  Pallas kernels: 0 us -> 33.4 us
  waiting for transfers between devices: 25.8 us -> 5.76 us
    dot_general x45 -> x0, matrix products: 99.3 us -> none  [the longest x5 22.4 us: shards(): jnp.dot(strain_map.T, weighted, precision=highest)]
    unnamed x228 -> x33, local copies, waits for them, and re-layouts: 64.8 us -> 2.88 us
    reshape x41 -> x0, local copies, waits for them, and re-layouts: 50.1 us -> none  [the longest x10 13.7 us: shards(): local_force.reshape(components, face_nodes, 3, elements)]
    all_to_all x15 -> x3, starting transfers between devices: 57.8 us -> 15.8 us  [exchange(): mixed = lax.all_to_all(cross, ('group', 'sub'), 0, 0, tiled=True)]
    ppermute x25 -> x6, starting transfers between devices: 45.4 us -> 7.24 us  [shifted(): return lax.ppermute(value, axis, pairs)]
    pallas_call x0 -> x7, Pallas kernels: none -> 33.4 us  [the longest x1 8.65 us: shards(): pl.pallas_call(functools.partial(inside, 5), grid=(inner // width,), out_...]
    slice x32 -> x0, local copies, waits for them, and re-layouts: 23.3 us -> none  [the longest x10 8.13 us: shards(): own_local = traces[:, :, 1:]]
    all_to_all x15 -> x0, other arithmetic: 19.9 us -> none  [route_traces(): lax.all_to_all(blocks[:, :, offset], 'sub', split_axis=2, concat_axis=2,...]
  transfers between devices with their start and end apart: 40 -> 9, of which waited for: 11 -> 3; matrix products, arithmetic and copies ran while one was open for 45% -> 1% of each run, Pallas kernels for 0% -> 29%
where the time goes in v1:
time: 66.6 us; the launch traced here: 66 us
  Pallas kernels  33.4 us (50%)
  starting transfers between devices  23.1 us (35%)
  waiting for transfers between devices  5.76 us (9%)
  local copies, waits for them, and re-layouts  2.88 us (4%)
  between operations  0.79 us (1%)
    all_to_all x3, starting transfers between devices, exchange(): mixed = lax.all_to_all(cross, ('group', 'sub'), 0, 0, tiled=True)  15.8 us
    pallas_call x1, Pallas kernels, shards(): pl.pallas_call(functools.partial(inside, 5), grid=(inner // width,), out_...  8.65 us
    ppermute x6, starting transfers between devices, shifted(): return lax.ppermute(value, axis, pairs)  7.24 us
    pallas_call x1, Pallas kernels, shards(): pl.pallas_call(functools.partial(prepare, sizes), out_shape=(struct((coun...  6.89 us
    pallas_call x1, Pallas kernels, shards(): pl.pallas_call(functools.partial(middle_steps, sizes), out_shape=(state_s...  5.04 us
    ppermute x6, waiting for transfers between devices, shifted(): return lax.ppermute(value, axis, pairs)  4.64 us
    pallas_call x1, Pallas kernels, shards(): pl.pallas_call(functools.partial(last_steps, sizes), grid=(1,), out_shape...  3.84 us
    pallas_call x1, Pallas kernels, shards(): pl.pallas_call(functools.partial(first_step, sizes), out_shape=(state_sha...  3.83 us
  transfers between devices with their start and end apart: 9, of which 3 were waited for; matrix products, arithmetic and copies ran while one was open for 1% of the time, Pallas kernels for 29%

profile of v1, /device:TPU:0, one launch (start us, length us, event | category | flops | bytes accessed | tf_op | source)
XLA Modules:
  0.0 66.0 jit_solution(5736911907092424127)
XLA Ops:
  0.6 0.0 copy-start.3
  0.6 1.7 %first_pack.1 = (f32[56,128]{1,0:T(8,128)}, f32[56,128]{1,0:T(8,128)}, f32[32,8,128]{2,1,0:T(8,128)}) custom-call(f32[3,35,1024]{2,1,0:T(8,128)} %disp.5, f32[1,1024]{1,0:T(1,128)} %bitcast.2), custom_call_target="tpu_custom_call" | custom-call | flops 1048576 | bytes 1048576 | tf_op jit(solution)/shard_map/first_pack/pallas_call | solution.py:559
  2.4 0.0 copy-start.15
  2.4 0.0 copy-start.14
  2.4 7.3 %all-to-all-start = ((f32[32,8,128]{2,1,0:T(8,128)}), f32[32,8,128]{2,1,0:T(8,128)S(1)}, u32[]{:S(2)}, u32[]{:S(2)}) async-start(f32[32,8,128]{2,1,0:T(8,128)} %get-tuple-element.32), calls=%async_computation | async-start | bytes 262144 | tf_op jit(solution)/shard_map/all_to_all | solution.py:520
  9.7 0.0 copy-done.15
  9.7 2.4 %collective-permute-start = (f32[56,128]{1,0:T(8,128)S(1)}, f32[56,128]{1,0:T(8,128)S(1)}, u32[]{:S(2)}, u32[]{:S(2)}) collective-permute-start(f32[56,128]{1,0:T(8,128)S(1)} %copy-done.15), channel_id=1, source_target_pairs={{0,7},{1,0},{2,1},{3,2},{4,3},{5,4},{6,5},{7,6},{8,15},{9,8},{10,9... | collective-permute-start | bytes 86024 | tf_op jit(solution)/shard_map/ppermute | solution.py:516
  12.2 0.0 copy-done.14
  12.2 0.0 collective-permute-start.1
  12.2 0.0 copy-done.3
  12.2 0.9 %copy.23.strain = f32[630,105]{1,0:T(8,128)} copy(f32[630,105]{0,1:T(8,128)S(1)} %copy-done.3) | data formatting | bytes 529200 | tf_op args[4]
  13.1 6.9 %prepare.1 = (bf16[6,128,256]{2,1,0:T(8,128)(2,1)}, bf16[6,128,256]{2,1,0:T(8,128)(2,1)}, bf16[256,144]{1,0:T(8,128)(2,1)}, bf16[128,144]{1,0:T(8,128)(2,1)}, bf16[48,144]{1,0:T(8,128)(2,1)}) custom-call(f32[630,105]{1,0:T(8,128)} %copy.23.strain, f32[15,15]{1,0:T(8,128)} %face_mass.1, f32[35,35]{1,0:T(8,128)} %mass_inverse.1, ...), custom_call_target="tpu_custom_call" | custom-call | flops 16777216 | bytes 1048576 | tf_op jit(solution)/shard_map/prepare/pallas_call | solution.py:569
  20.0 3.4 %start_rim.1 = (f32[128,512]{1,0:T(8,128)}, f32[128,512]{1,0:T(8,128)}, f32[24,512]{1,0:T(8,128)}, s32[8,512]{1,0:T(8,128)}, f32[8,512]{1,0:T(8,128)}) custom-call(f32[3,35,1024]{2,1,0:T(8,128)} %disp.5, f32[3,35,1024]{2,1,0:T(8,128)} %vel.3, s32[2,3072]{1,0:T(2,128)} %link3.1, f32[4,3072]{1,0:T(4,128)} %geo3.1, f32[6,1024]{1,0:T(8,128)} %weights.3, ...), custom_call_target="tpu_custom_call" | custom-call | flops 16777216 | bytes 1048576 | tf_op jit(solution)/shard_map/start_rim/pallas_call | solution.py:582
  23.4 0.0 collective-permute-done.upper_in
  23.4 0.0 copy-start.8
  23.4 0.0 collective-permute-done.1.lower_in
  23.4 0.0 copy-start.9
  23.5 0.0 all-to-all-done.cross_in
  23.5 0.0 copy-start
  23.5 0.5 copy-done.8
  24.0 0.0 copy-done.9
  24.1 0.1 copy-done
  24.1 3.8 %first_step.1 = (f32[128,512]{1,0:T(8,128)}, f32[128,512]{1,0:T(8,128)}, f32[48,512]{1,0:T(8,128)}, f32[8,512]{1,0:T(8,128)}, f32[96,128]{1,0:T(8,128)}, /*index=5*/f32[96,128]{1,0:T(8,128)}, f32[32,8,128]{2,1,0:T(8,128)}) custom-call(f32[56,128]{1,0:T(8,128)} %copy-done.8, f32[56,128]{1,0:T(8,128)} %copy-done.9, f32[32,8,128]{2,1,0:T(8,128)} %copy-done, ...), custom_call_target="tpu_custom_call" | custom-call | flops 16777216 | bytes 1048576 | tf_op jit(solution)/shard_map/first_step/pallas_call | solution.py:612
  27.9 0.0 copy-start.13
  28.0 0.0 copy-start.11
  28.0 5.8 %all-to-all-start.1 = ((f32[32,8,128]{2,1,0:T(8,128)}), f32[32,8,128]{2,1,0:T(8,128)S(1)}, u32[]{:S(2)}, u32[]{:S(2)}) async-start(f32[32,8,128]{2,1,0:T(8,128)} %get-tuple-element.44), calls=%async_computation.1 | async-start | bytes 262144 | tf_op jit(solution)/shard_map/all_to_all | solution.py:520
  33.8 0.0 copy-done.13
  33.8 2.4 %collective-permute-start.2 = (f32[96,128]{1,0:T(8,128)S(1)}, f32[96,128]{1,0:T(8,128)S(1)}, u32[]{:S(2)}, u32[]{:S(2)}) collective-permute-start(f32[96,128]{1,0:T(8,128)S(1)} %copy-done.13), channel_id=1, source_target_pairs={{0,7},{1,0},{2,1},{3,2},{4,3},{5,4},{6,5},{7,6},{8,15},{9,8},{10,9... | collective-permute-start | bytes 147464 | tf_op jit(solution)/shard_map/ppermute | solution.py:516
  36.2 0.0 copy-done.11
  36.2 0.0 collective-permute-start.3
  36.2 1.8 %collective-permute-done.2.upper_in = f32[96,128]{1,0:T(8,128)S(1)} collective-permute-done((f32[96,128]{1,0:T(8,128)S(1)}, f32[96,128]{1,0:T(8,128)S(1)}, u32[]{:S(2)}, u32[]{:S(2)}) %collective-permute-start.2) | collective-permute-done | bytes 49184 | tf_op jit(solution)/shard_map/ppermute | solution.py:516
  38.0 0.0 copy-start.6
  38.0 2.8 %collective-permute-done.3.lower_in = f32[96,128]{1,0:T(8,128)S(1)} collective-permute-done((f32[96,128]{1,0:T(8,128)S(1)}, f32[96,128]{1,0:T(8,128)S(1)}, u32[]{:S(2)}, u32[]{:S(2)}) %collective-permute-start.3) | collective-permute-done | bytes 49184 | tf_op jit(solution)/shard_map/ppermute | solution.py:516
  40.9 0.0 copy-start.7
  40.9 1.1 %all-to-all-done.1.cross_in = f32[32,8,128]{2,1,0:T(8,128)S(1)} async-done(((f32[32,8,128]{2,1,0:T(8,128)}), f32[32,8,128]{2,1,0:T(8,128)S(1)}, u32[]{:S(2)}, u32[]{:S(2)}) %all-to-all-start.1) | async-done | bytes 131104 | tf_op jit(solution)/shard_map/all_to_all | solution.py:520
  42.0 0.0 copy-start.2
  42.0 0.0 copy-done.6
  42.0 0.0 copy-done.7
  42.0 0.6 copy-done.2
  42.6 5.0 %middle_steps.1 = (f32[128,512]{1,0:T(8,128)}, f32[128,512]{1,0:T(8,128)}, f32[48,512]{1,0:T(8,128)}, f32[96,128]{1,0:T(8,128)}, f32[96,128]{1,0:T(8,128)}, /*index=5*/f32[32,8,128]{2,1,0:T(8,128)}) custom-call(f32[96,128]{1,0:T(8,128)} %copy-done.6, f32[96,128]{1,0:T(8,128)} %copy-done.7, f32[32,8,128]{2,1,0:T(8,128)} %copy-done.2, ...), custom_call_target="tpu_custom_call" | custom-call | flops 16777216 | bytes 1048576 | tf_op jit(solution)/shard_map/middle_steps/pallas_call | solution.py:663
  47.7 0.0 copy-start.12
  47.7 0.0 copy-start.10
  47.7 2.7 %all-to-all-start.2 = ((f32[32,8,128]{2,1,0:T(8,128)}), f32[32,8,128]{2,1,0:T(8,128)S(1)}, u32[]{:S(2)}, u32[]{:S(2)}) async-start(f32[32,8,128]{2,1,0:T(8,128)} %get-tuple-element.52), calls=%async_computation.2 | async-start | bytes 262144 | tf_op jit(solution)/shard_map/all_to_all | solution.py:520
  50.4 0.0 copy-done.12
  50.4 2.3 %collective-permute-start.4 = (f32[96,128]{1,0:T(8,128)S(1)}, f32[96,128]{1,0:T(8,128)S(1)}, u32[]{:S(2)}, u32[]{:S(2)}) collective-permute-start(f32[96,128]{1,0:T(8,128)S(1)} %copy-done.12), channel_id=1, source_target_pairs={{0,7},{1,0},{2,1},{3,2},{4,3},{5,4},{6,5},{7,6},{8,15},{9,8},{10,9... | collective-permute-start | bytes 147464 | tf_op jit(solution)/shard_map/ppermute | solution.py:516
  52.8 0.0 copy-done.10
  52.8 0.0 collective-permute-start.5
  52.8 8.7 %inside.1 = (f32[3,35,1024]{2,1,0:T(8,128)}, f32[3,35,1024]{2,1,0:T(8,128)}) custom-call(f32[3,35,1024]{2,1,0:T(8,128)} %disp.5, f32[3,35,1024]{2,1,0:T(8,128)} %vel.3, s32[2,3072]{1,0:T(2,128)} %link3.1, s32[2,3072]{1,0:T(2,128)} %link3.1, s32[2,3072]{1,0:T(2,128)} %link3.1, f32[4,3072]{1,0:T(4,128)} %geo3.1, f32[4,3072]{1,0:T(4,128)} %geo3.1, ...), custom_call_target="tpu_custom_call" | custom-call | flops 67108864 | bytes 1048576 | tf_op jit(solution)/shard_map/inside/pallas_call | solution.py:632
  61.4 0.0 collective-permute-done.4.upper_in
  61.4 0.0 copy-start.4
  61.4 0.0 collective-permute-done.5.lower_in
  61.4 0.0 copy-start.5
  61.5 0.0 all-to-all-done.2.cross_in
  61.5 0.0 copy-start.1
  61.5 0.6 copy-done.4
  62.0 0.0 copy-done.5
  62.1 0.0 copy-done.1
  62.1 3.8 %last_steps.1 = (f32[3,35,1024]{2,1,0:T(8,128)}, f32[3,35,1024]{2,1,0:T(8,128)}) custom-call(f32[96,128]{1,0:T(8,128)} %copy-done.4, f32[96,128]{1,0:T(8,128)} %copy-done.5, f32[32,8,128]{2,1,0:T(8,128)} %copy-done.1, f32[128,512]{1,0:T(8,128)} %get-tuple-element.53.field, ...), custom_call_target="tpu_custom_call", output_to_operand_aliasing={{0}: (15, {}), {1}: (16, {})} | custom-call | flops 16777216 | bytes 1048576 | tf_op jit(solution)/shard_map/last_steps/pallas_call | solution.py:672
Async XLA Ops:
  0.6 11.6 %copy-start.3 = (f32[630,105]{0,1:T(8,128)S(1)}, f32[630,105]{0,1:T(8,128)}, u32[]{:S(2)}) copy-start(f32[630,105]{0,1:T(8,128)} %param.23) | copy-start | bytes 793804
  2.4 7.3 %copy-start.15 = (f32[56,128]{1,0:T(8,128)S(1)}, f32[56,128]{1,0:T(8,128)}, u32[]{:S(2)}) copy-start(f32[56,128]{1,0:T(8,128)} %get-tuple-element.30) | copy-start | bytes 86020
  2.4 9.8 %copy-start.14 = (f32[56,128]{1,0:T(8,128)S(1)}, f32[56,128]{1,0:T(8,128)}, u32[]{:S(2)}) copy-start(f32[56,128]{1,0:T(8,128)} %get-tuple-element.31) | copy-start | bytes 86020
  2.4 21.1 %all-to-all-start = ((f32[32,8,128]{2,1,0:T(8,128)}), f32[32,8,128]{2,1,0:T(8,128)S(1)}, u32[]{:S(2)}, u32[]{:S(2)}) async-start(f32[32,8,128]{2,1,0:T(8,128)} %get-tuple-element.32), calls=%async_computation | async-start | bytes 262144 | tf_op jit(solution)/shard_map/all_to_all | solution.py:520
  9.7 13.7 %collective-permute-start = (f32[56,128]{1,0:T(8,128)S(1)}, f32[56,128]{1,0:T(8,128)S(1)}, u32[]{:S(2)}, u32[]{:S(2)}) collective-permute-start(f32[56,128]{1,0:T(8,128)S(1)} %copy-done.15), channel_id=1, source_target_pairs={{0,7},{1,0},{2,1},{3,2},{4,3},{5,4},{6,5},{7,6},{8,15},{9,8},{10,9... | collective-permute-start | bytes 86024 | tf_op jit(solution)/shard_map/ppermute | solution.py:516
  12.2 11.3 %collective-permute-start.1 = (f32[56,128]{1,0:T(8,128)S(1)}, f32[56,128]{1,0:T(8,128)S(1)}, u32[]{:S(2)}, u32[]{:S(2)}) collective-permute-start(f32[56,128]{1,0:T(8,128)S(1)} %copy-done.14), channel_id=1, source_target_pairs={{0,1},{1,2},{2,3},{3,4},{4,5},{5,6},{6,7},{7,0},{8,9},{9,10},{10,1... | collective-permute-start | bytes 86024 | tf_op jit(solution)/shard_map/ppermute | solution.py:516
  23.4 0.6 copy-start.8
  23.4 0.6 copy-start.9
  23.5 0.7 copy-start
  27.9 5.8 %copy-start.13 = (f32[96,128]{1,0:T(8,128)S(1)}, f32[96,128]{1,0:T(8,128)}, u32[]{:S(2)}) copy-start(f32[96,128]{1,0:T(8,128)} %get-tuple-element.42) | copy-start | bytes 147460
  28.0 8.3 %copy-start.11 = (f32[96,128]{1,0:T(8,128)S(1)}, f32[96,128]{1,0:T(8,128)}, u32[]{:S(2)}) copy-start(f32[96,128]{1,0:T(8,128)} %get-tuple-element.43) | copy-start | bytes 147460
  28.0 14.0 %all-to-all-start.1 = ((f32[32,8,128]{2,1,0:T(8,128)}), f32[32,8,128]{2,1,0:T(8,128)S(1)}, u32[]{:S(2)}, u32[]{:S(2)}) async-start(f32[32,8,128]{2,1,0:T(8,128)} %get-tuple-element.44), calls=%async_computation.1 | async-start | bytes 262144 | tf_op jit(solution)/shard_map/all_to_all | solution.py:520
  33.8 4.2 %collective-permute-start.2 = (f32[96,128]{1,0:T(8,128)S(1)}, f32[96,128]{1,0:T(8,128)S(1)}, u32[]{:S(2)}, u32[]{:S(2)}) collective-permute-start(f32[96,128]{1,0:T(8,128)S(1)} %copy-done.13), channel_id=1, source_target_pairs={{0,7},{1,0},{2,1},{3,2},{4,3},{5,4},{6,5},{7,6},{8,15},{9,8},{10,9... | collective-permute-start | bytes 147464 | tf_op jit(solution)/shard_map/ppermute | solution.py:516
  36.2 4.6 %collective-permute-start.3 = (f32[96,128]{1,0:T(8,128)S(1)}, f32[96,128]{1,0:T(8,128)S(1)}, u32[]{:S(2)}, u32[]{:S(2)}) collective-permute-start(f32[96,128]{1,0:T(8,128)S(1)} %copy-done.11), channel_id=1, source_target_pairs={{0,1},{1,2},{2,3},{3,4},{4,5},{5,6},{6,7},{7,0},{8,9},{9,10},{10,1... | collective-permute-start | bytes 147464 | tf_op jit(solution)/shard_map/ppermute | solution.py:516
  38.0 4.0 %copy-start.6 = (f32[96,128]{1,0:T(8,128)}, f32[96,128]{1,0:T(8,128)S(1)}, u32[]{:S(2)}) copy-start(f32[96,128]{1,0:T(8,128)S(1)} %collective-permute-done.2.upper_in) | copy-start | bytes 147460
  40.9 1.1 %copy-start.7 = (f32[96,128]{1,0:T(8,128)}, f32[96,128]{1,0:T(8,128)S(1)}, u32[]{:S(2)}) copy-start(f32[96,128]{1,0:T(8,128)S(1)} %collective-permute-done.3.lower_in) | copy-start | bytes 147460
  42.0 0.7 copy-start.2
  47.7 2.7 %copy-start.12 = (f32[96,128]{1,0:T(8,128)S(1)}, f32[96,128]{1,0:T(8,128)}, u32[]{:S(2)}) copy-start(f32[96,128]{1,0:T(8,128)} %get-tuple-element.50) | copy-start | bytes 147460
  47.7 5.1 %copy-start.10 = (f32[96,128]{1,0:T(8,128)S(1)}, f32[96,128]{1,0:T(8,128)}, u32[]{:S(2)}) copy-start(f32[96,128]{1,0:T(8,128)} %get-tuple-element.51) | copy-start | bytes 147460
  47.7 13.8 %all-to-all-start.2 = ((f32[32,8,128]{2,1,0:T(8,128)}), f32[32,8,128]{2,1,0:T(8,128)S(1)}, u32[]{:S(2)}, u32[]{:S(2)}) async-start(f32[32,8,128]{2,1,0:T(8,128)} %get-tuple-element.52), calls=%async_computation.2 | async-start | bytes 262144 | tf_op jit(solution)/shard_map/all_to_all | solution.py:520
  50.4 11.0 %collective-permute-start.4 = (f32[96,128]{1,0:T(8,128)S(1)}, f32[96,128]{1,0:T(8,128)S(1)}, u32[]{:S(2)}, u32[]{:S(2)}) collective-permute-start(f32[96,128]{1,0:T(8,128)S(1)} %copy-done.12), channel_id=1, source_target_pairs={{0,7},{1,0},{2,1},{3,2},{4,3},{5,4},{6,5},{7,6},{8,15},{9,8},{10,9... | collective-permute-start | bytes 147464 | tf_op jit(solution)/shard_map/ppermute | solution.py:516
  52.8 8.7 %collective-permute-start.5 = (f32[96,128]{1,0:T(8,128)S(1)}, f32[96,128]{1,0:T(8,128)S(1)}, u32[]{:S(2)}, u32[]{:S(2)}) collective-permute-start(f32[96,128]{1,0:T(8,128)S(1)} %copy-done.10), channel_id=1, source_target_pairs={{0,1},{1,2},{2,3},{3,4},{4,5},{5,6},{6,7},{7,0},{8,9},{9,10},{10,1... | collective-permute-start | bytes 147464 | tf_op jit(solution)/shard_map/ppermute | solution.py:516
  61.4 0.6 copy-start.4
  61.4 0.6 copy-start.5
  61.5 0.7 copy-start.1

commit v2 on v1

--- a/solution.py
+++ b/solution.py
@@ -11,10 +11,12 @@
 
 BLOCK = 128
 PAD = 40
-ROWS = 128
+ROWS = 3 * PAD
+DEPTH = 128
 FACE = 16
 TRACE = 3 * FACE
 TILE = 256
+VMEM_LIMIT = 20 << 20
 
 shear_weight = 0.5
 opening_scale = 4.0
@@ -42,47 +44,47 @@
 def tables():
     table = face_table()
     nodes = table.shape[2]
-    spread = np.zeros((3 * nodes, ROWS), np.float32)
-    rows = np.zeros((ROWS, nodes), np.float32)
-    for c in range(3):
-        for n in range(nodes):
-            spread[c * nodes + n, c * PAD + n] = 1.0
-            rows[c * PAD + n, n] = 1.0
-    place = np.zeros((3 * TRACE, 15), np.float32)
+    place = np.zeros((9 * TRACE, 15), np.float32)
     lift = np.zeros((ROWS, 3 * TRACE), np.float32)
     lift0 = np.zeros((ROWS, TRACE), np.float32)
     for c in range(3):
         for i in range(15):
-            for k in range(3):
+            for k in range(9):
                 place[k * TRACE + c * FACE + i, i] = 1.0
-                for n in range(nodes):
+            for n in range(nodes):
+                for k in range(3):
                     lift[c * PAD + n, k * TRACE + c * FACE + i] = table[k + 1, i, n]
-            for n in range(nodes):
                 lift0[c * PAD + n, c * FACE + i] = table[0, i, n]
-    pick = np.concatenate([lift.T, lift.T], axis=1)
-    return spread, rows, place, lift, lift0, pick
+    pick = np.zeros((3 * TRACE, 2 * DEPTH), np.float32)
+    pick[:, 0:ROWS] = lift.T
+    pick[:, DEPTH : DEPTH + ROWS] = lift.T
+    return place, lift, lift0, pick
 
 
 def dot(a, b):
     return lax.dot_general(a, b, (((1,), (0,)), ((), ())), preferred_element_type=f32)
 
 
-def dot_full(a, b):
-    return lax.dot_general(
-        a, b, (((1,), (0,)), ((), ())), precision=highest, preferred_element_type=f32
-    )
-
-
-def dot_full_t(a, b):
-    return lax.dot_general(
-        a, b, (((1,), (1,)), ((), ())), precision=highest, preferred_element_type=f32
-    )
+def dot_t(a, b):
+    return lax.dot_general(a, b, (((1,), (1,)), ((), ())), preferred_element_type=f32)
 
 
 def pieces(value):
     high = value.astype(bf16)
     low = (value - high.astype(f32)).astype(bf16)
     return high, low
+
+
+def dot_pieces(a, b, product=dot):
+    a0, a1 = pieces(a)
+    b0, b1 = pieces(b)
+    return product(a0, b0) + (product(a0, b1) + product(a1, b0))
+
+
+def dot_exact(table, b):
+    table = table.astype(bf16)
+    b0, b1 = pieces(b)
+    return dot(table, b0) + dot(table, b1)
 
 
 def traction(jump, normal, weight0, weight1):
@@ -114,42 +116,53 @@
     coef[15 : 15 + count, :] = weights * inverse
 
 
-def local_change(field, at, coef, index, ops):
-    high_op, low_op, pick, lift = ops
-    lanes = pl.ds(at, TILE)
-    high, low = pieces(field[:, lanes])
-    both = jnp.concatenate([high, low], axis=0)
-    total = None
-    for m in range(high_op.shape[0]):
-        part = dot(high_op[m], both) + dot(low_op[m], both)
-        part = part * coef[15 + m : 16 + m, lanes]
-        total = part if total is None else total + part
-    traces = dot(pick[...], both)
-    halves = []
-    for half in range(TILE // BLOCK):
-        start = at + half * BLOCK
-        part = traces[:, half * BLOCK : (half + 1) * BLOCK]
-        forces = []
-        for q in range(3):
-            where = jnp.broadcast_to(index[q : q + 1, pl.ds(start, BLOCK)], (TRACE, BLOCK))
-            side = index[3 + q : 4 + q, pl.ds(start, BLOCK)]
-            found = [
-                jnp.take_along_axis(
-                    part[k * TRACE : (k + 1) * TRACE], where, axis=1, mode="promise_in_bounds"
-                )
-                for k in range(3)
-            ]
-            paired = jnp.where(side == 0, found[0], jnp.where(side == 1, found[1], found[2]))
-            jump = paired - part[q * TRACE : (q + 1) * TRACE]
-            rows = [coef[5 * q + r : 5 * q + r + 1, pl.ds(start, BLOCK)] for r in range(5)]
-            forces += traction(
-                [jump[c * FACE : (c + 1) * FACE] for c in range(3)], rows[0:3], rows[3], rows[4]
-            )
-        halves.append(jnp.concatenate(forces, axis=0))
-    high, low = pieces(jnp.concatenate(halves, axis=1))
-    first = dot(lift[...], high)
-    second = dot(lift[0:ROWS, :], low)
-    return total + (first[0:ROWS] + first[ROWS : 2 * ROWS] + second)
+def local_changes(field, starts, coef, index, ops):
+    strain_op, pick, lift = ops
+    blocks = strain_op.shape[0] // ROWS
+    factors = []
+    for at in starts:
+        value = jnp.concatenate(
+            [field[:, at : at + TILE], jnp.zeros((DEPTH - ROWS, TILE), f32)], axis=0
+        )
+        high, low = pieces(value)
+        factors.append(jnp.concatenate([high, low, high], axis=0))
+    traces = [dot(pick[...], factor[0 : 2 * DEPTH]) for factor in factors]
+    strains = [dot(strain_op[...], factor) for factor in factors]
+    forces = []
+    for at, trace in zip(starts, traces):
+        halves = []
+        for half in range(TILE // BLOCK):
+            lanes = slice(at + half * BLOCK, at + (half + 1) * BLOCK)
+            part = trace[:, half * BLOCK : (half + 1) * BLOCK]
+            rows = []
+            for q in range(3):
+                where = jnp.broadcast_to(index[q : q + 1, lanes], (TRACE, BLOCK))
+                side = index[3 + q : 4 + q, lanes]
+                found = [
+                    jnp.take_along_axis(
+                        part[k * TRACE : (k + 1) * TRACE], where, axis=1, mode="promise_in_bounds"
+                    )
+                    for k in range(3)
+                ]
+                paired = jnp.where(side == 0, found[0], jnp.where(side == 1, found[1], found[2]))
+                jump = paired - part[q * TRACE : (q + 1) * TRACE]
+                weights = [coef[5 * q + r : 5 * q + r + 1, lanes] for r in range(5)]
+                rows += traction(split_rows(jump), weights[0:3], weights[3], weights[4])
+            halves.append(jnp.concatenate(rows, axis=0))
+        forces.append(jnp.concatenate(halves, axis=1))
+    results = []
+    for at, strain, force in zip(starts, strains, forces):
+        high, low = pieces(force)
+        total = dot(lift[...], jnp.concatenate([high, low, high], axis=0))
+        parts = []
+        for g in range(ROWS // 8):
+            part = total[g * 8 : (g + 1) * 8]
+            for m in range(blocks):
+                first = (g * blocks + m) * 8
+                part = part + coef[15 + m : 16 + m, at : at + TILE] * strain[first : first + 8]
+            parts.append(part)
+        results.append(jnp.concatenate(parts, axis=0))
+    return results
 
 
 def load_state(source, target):
@@ -217,51 +230,81 @@
 
 
 def prepare(
-    sizes,
     strain,
     face_mass,
     mass_inverse,
-    spread,
-    rows,
     place,
     lift,
     lift0,
-    high_op,
-    low_op,
+    strain_op,
     lift_op,
     lift0_op,
     trace_op,
+    wide,
+    corner,
+    inverse,
+    first,
+    second,
 ):
-    size = strain.shape[1]
-    row = lax.broadcasted_iota(jnp.int32, (ROWS, ROWS), 0)
-    col = lax.broadcasted_iota(jnp.int32, (ROWS, ROWS), 1)
-    inverse = dot_full_t(dot_full(rows[...], mass_inverse[...]), rows[...])
-    inverse = jnp.where(lax.div(row, PAD) == lax.div(col, PAD), inverse, 0.0)
-    inverse = inverse * (time_step * time_step)
-    for m in range(high_op.shape[0]):
-        block = dot_full(strain[m * size : (m + 1) * size, :], spread[...])
-        value = -dot_full(dot_full_t(inverse, block), block)
-        high, low = pieces(value)
-        high_op[m] = jnp.concatenate([high, high], axis=1)
-        low_op[m] = jnp.concatenate([low, low], axis=1)
-    wide = 3 * TRACE
-    row = lax.broadcasted_iota(jnp.int32, (wide, wide), 0)
-    col = lax.broadcasted_iota(jnp.int32, (wide, wide), 1)
-    mass = dot_full_t(dot_full(place[...], face_mass[...]), place[...])
+    nodes = mass_inverse.shape[0]
+    size = 3 * nodes
+    count = strain.shape[1]
+    blocks = count // size
+    wide[...] = jnp.zeros_like(wide)
+    corner[...] = jnp.zeros_like(corner)
+    corner[0:nodes, 0:nodes] = (time_step * time_step) * mass_inverse[...]
+    inverse[...] = jnp.zeros_like(inverse)
+    for c in range(3):
+        wide[c * PAD : c * PAD + nodes, 0:count] = strain[c * nodes : (c + 1) * nodes, :]
+        inverse[c * PAD : (c + 1) * PAD, :] = pltpu.roll(corner[...], c * PAD, 1)
+    rows0, rows1 = pieces(wide[...])
+    base = inverse[...]
+    base0, base1 = pieces(base)
+    left = dot(base0, rows0) + (dot(base0, rows1) + dot(base1, rows0))
+    left0, left1 = pieces(left)
+    for m in range(blocks):
+        begin = m * size // DEPTH * DEPTH
+        end = min(begin + 2 * DEPTH, wide.shape[1])
+        lane = begin + lax.broadcasted_iota(jnp.int32, (DEPTH, end - begin), 1)
+        inside = (lane >= m * size) & (lane < (m + 1) * size)
+        cut0 = jnp.where(inside, left[:, begin:end], 0.0)
+        cut0, cut1 = pieces(cut0)
+        value = -(
+            dot_t(cut0, rows0[:, begin:end])
+            + (dot_t(cut0, rows1[:, begin:end]) + dot_t(cut1, rows0[:, begin:end]))
+        )
+        high = value.astype(bf16).astype(f32)
+        low = value - high
+        for g in range(ROWS // 8):
+            at = (g * blocks + m) * 8
+            first[at : at + 8, :] = high[g * 8 : (g + 1) * 8]
+            second[at : at + 8, :] = low[g * 8 : (g + 1) * 8]
+    high = first[...].astype(bf16)
+    strain_op[:, 0:DEPTH] = high
+    strain_op[:, DEPTH : 2 * DEPTH] = high
+    strain_op[:, 2 * DEPTH :] = second[...].astype(bf16)
+
+    row = lax.broadcasted_iota(jnp.int32, (3 * TRACE, 9 * TRACE), 0)
+    col = lax.broadcasted_iota(jnp.int32, (3 * TRACE, 9 * TRACE), 1)
+    part0, part1 = pieces(dot_exact(place[0 : 3 * TRACE, :], face_mass[...]))
+    spread = place[...].astype(bf16)
+    mass = dot_t(part0, spread) + dot_t(part1, spread)
     same = lax.rem(lax.div(row, FACE), 3) == lax.rem(lax.div(col, FACE), 3)
     mass = jnp.where(same, mass, 0.0)
-    inner = jnp.where(lax.div(row, TRACE) == lax.div(col, TRACE), mass, 0.0)
-    value = dot_full(inverse, dot_full(lift[...], inner))
-    high, low = pieces(value)
-    lift_op[0:ROWS, :] = high
-    lift_op[ROWS : 2 * ROWS, :] = low
-    value = dot_full(inverse, dot_full(lift0[...], mass[0:TRACE, :]))
+    each = jnp.where(lax.div(row, TRACE) == lax.rem(lax.div(col, TRACE), 3), mass, 0.0)
+    zeros = jnp.zeros((DEPTH - ROWS, 9 * TRACE), f32)
+
+    def lifted(table, factor):
+        value = jnp.concatenate([dot_exact(table[...], factor), zeros[:, 0 : factor.shape[1]]], axis=0)
+        return dot_pieces(base, value)[0:ROWS]
 
     def three(value):
         high = value.astype(bf16).astype(f32)
         col = lax.broadcasted_iota(jnp.int32, value.shape, 1)
-        return jnp.where(col < 2 * TRACE, high, value - high).astype(bf16)
-
+        return jnp.where(col < value.shape[1] // 3 * 2, high, value - high).astype(bf16)
+
+    lift_op[...] = three(lifted(lift, each))
+    value = lifted(lift0, mass[0:TRACE, 0 : 3 * TRACE])
     lift0_op[...] = three(value)
     trace_op[...] = three(
         jnp.concatenate([value[c * PAD : c * PAD + FACE] for c in range(3)], axis=0)
@@ -280,8 +323,7 @@
     next_geometry,
     cross_links,
     cross_geometry,
-    high_op,
-    low_op,
+    strain_op,
     pick,
     lift_op,
     field_out,
@@ -315,12 +357,11 @@
     rim[5:6, :] = rim[6:7, :] * (1.0 / inverse)
     load_state(disp, field_out)
     load_state(vel, vel_out)
-    ops = (high_op, low_op, pick, lift_op)
-    for at in range(0, lanes, TILE):
+    ops = (strain_op, pick, lift_op)
+    starts = range(0, lanes, TILE)
+    for at, change in zip(starts, local_changes(field_out, starts, coef, index, ops)):
         span = pl.ds(at, TILE)
-        vel_out[:, span] = time_step * vel_out[:, span] + local_change(
-            field_out, at, coef, index, ops
-        )
+        vel_out[:, span] = time_step * vel_out[:, span] + change
 
 
 def first_step(
@@ -333,8 +374,7 @@
     coef,
     index,
     rim,
-    high_op,
-    low_op,
+    strain_op,
     pick,
     lift_op,
     lift0_op,
@@ -358,7 +398,7 @@
     speed = vel[...] + change
     vel_out[...] = speed
     field_out[...] = field[...] + speed
-    send_two(sizes, field_out, vel_out, own_out, coef, index, (high_op, low_op, pick, lift_op), upper, lower, cross)
+    send_two(sizes, field_out, vel_out, own_out, coef, index, (strain_op, pick, lift_op), upper, lower, cross)
 
 
 def send_two(sizes, field_out, vel_out, own_out, coef, index, ops, upper, lower, cross):
@@ -366,9 +406,10 @@
     every = slice(None)
     first = jnp.concatenate(trace_of(field_out, every), axis=0)
     own_out[...] = first
-    for at in range(0, lanes, TILE):
+    starts = range(0, lanes, TILE)
+    for at, change in zip(starts, local_changes(field_out, starts, coef, index, ops)):
         span = pl.ds(at, TILE)
-        speed = vel_out[:, span] + local_change(field_out, at, coef, index, ops)
+        speed = vel_out[:, span] + change
         vel_out[:, span] = speed
         field_out[:, span] = field_out[:, span] + speed
     second = jnp.concatenate(trace_of(field_out, every), axis=0)
@@ -386,12 +427,11 @@
     change = times_lift0(lift0_op, pull * rim[5:6, :])
     vel_out[...] = vel[...] + change
     field_out[...] = field[...] + change
-    change = times_lift0(lift0_op, pull_later * rim[5:6, :])
-    for at in range(0, lanes, TILE):
+    later = times_lift0(lift0_op, pull_later * rim[5:6, :])
+    starts = range(0, lanes, TILE)
+    for at, change in zip(starts, local_changes(field_out, starts, coef, index, ops)):
         span = pl.ds(at, TILE)
-        speed = vel_out[:, span] + (
-            local_change(field_out, at, coef, index, ops) + change[:, at : at + TILE]
-        )
+        speed = vel_out[:, span] + (change + later[:, at : at + TILE])
         vel_out[:, span] = speed
         field_out[:, span] = field_out[:, span] + speed
 
@@ -407,20 +447,15 @@
     coef,
     index,
     rim,
-    high_op,
-    low_op,
+    strain_op,
     pick,
     lift_op,
     lift0_op,
     trace_op,
-    field_out,
-    vel_out,
-    own_out,
-    upper,
-    lower,
-    cross,
+    *rest,
 ):
-    ops = (high_op, low_op, pick, lift_op)
+    field_out, vel_out, own_out, upper, lower, cross = rest[-6:]
+    ops = (strain_op, pick, lift_op)
     take_two(sizes, upper_in, lower_in, cross_in, field, vel, own, coef, index, rim, ops, lift0_op, trace_op, field_out, vel_out)
     send_two(sizes, field_out, vel_out, own_out, coef, index, ops, upper, lower, cross)
 
@@ -436,8 +471,7 @@
     coef,
     index,
     rim,
-    high_op,
-    low_op,
+    strain_op,
     pick,
     lift_op,
     lift0_op,
@@ -445,7 +479,7 @@
     *rest,
 ):
     disp_out, vel_out, field_new, vel_new = rest[-4:]
-    ops = (high_op, low_op, pick, lift_op)
+    ops = (strain_op, pick, lift_op)
     take_two(sizes, upper_in, lower_in, cross_in, field, vel, own, coef, index, rim, ops, lift0_op, trace_op, field_new, vel_new)
     store_state(field_new, vel_new, disp_out, vel_out)
 
@@ -457,7 +491,21 @@
         vel_out[c] = (1.0 / time_step) * vel[c * PAD : c * PAD + nodes, :]
 
 
-def inside(
+def advance(steps, field, speed, coef, index, ops):
+    starts = range(0, field.shape[1], TILE)
+
+    def step(_, carry):
+        for at, change in zip(starts, local_changes(field, starts, coef, index, ops)):
+            span = pl.ds(at, TILE)
+            new = speed[:, span] + change
+            speed[:, span] = new
+            field[:, span] = field[:, span] + new
+        return carry
+
+    lax.fori_loop(0, steps, step, 0)
+
+
+def inside_first(
     steps,
     disp,
     vel,
@@ -469,12 +517,10 @@
     geo3,
     weights,
     jac,
-    high_op,
-    low_op,
+    strain_op,
     pick,
     lift_op,
-    disp_out,
-    vel_out,
+    after,
     field,
     speed,
     coef,
@@ -488,17 +534,15 @@
     load_state(disp, field)
     load_state(vel, speed)
     speed[...] = time_step * speed[...]
-    ops = (high_op, low_op, pick, lift_op)
-
-    def step(_, carry):
-        for at in range(0, field.shape[1], TILE):
-            span = pl.ds(at, TILE)
-            new = speed[:, span] + local_change(field, at, coef, index, ops)
-            speed[:, span] = new
-            field[:, span] = field[:, span] + new
-        return carry
-
-    lax.fori_loop(0, steps, step, 0)
+    advance(steps, field, speed, coef, index, (strain_op, pick, lift_op))
+
+
+def inside_last(
+    steps, field_in, speed_in, coef, index, strain_op, pick, lift_op, after, disp_out, vel_out, field, speed
+):
+    field[...] = field_in[...]
+    speed[...] = speed_in[...]
+    advance(steps, field, speed, coef, index, (strain_op, pick, lift_op))
     store_state(field, speed, disp_out, vel_out)
 
 
@@ -544,14 +588,16 @@
     shared = neighbour_links.shape[1]
     lanes = math.ceil((2 * shared + slots) / TILE) * TILE
     sizes = (shared, groups, places, lanes)
-    spread, rows, place, lift, lift0, pick = (jnp.asarray(t) for t in tables())
+    place, lift, lift0, pick = (jnp.asarray(t) for t in tables())
     pick = pick.astype(bf16)
     jac = jacobian.reshape(1, elements)
     cross_row = cross_links.reshape(1, slots)
     state_shape = struct((ROWS, lanes))
     vmem = pl.BlockSpec(memory_space=pltpu.VMEM)
+    anywhere = pl.BlockSpec(memory_space=pl.ANY)
     part = pl.BlockSpec((components, nodes, lanes), lambda i: (0, 0, 0))
     devices = groups * places
+    params = pltpu.CompilerParams(vmem_limit_bytes=VMEM_LIMIT)
 
     def messages(height):
         return (struct((height, shared)), struct((height, shared)), struct((devices, 8, BLOCK)))
@@ -562,22 +608,32 @@
         out_shape=messages(TRACE + 8),
         in_specs=[part, vmem],
         cost_estimate=cost(1 << 20),
+        compiler_params=params,
         name="first_pack",
     )(displacement, jac)
     arrived = exchange(*sends)
 
-    high_op, low_op, lift_op, lift0_op, trace_op = pl.pallas_call(
-        functools.partial(prepare, sizes),
+    wide = math.ceil(strain_map.shape[0] / DEPTH) * DEPTH
+    strain_op, lift_op, lift0_op, trace_op = pl.pallas_call(
+        prepare,
         out_shape=(
-            struct((count, ROWS, 2 * ROWS), bf16),
-            struct((count, ROWS, 2 * ROWS), bf16),
-            struct((2 * ROWS, 3 * TRACE), bf16),
+            struct((count * ROWS, 3 * DEPTH), bf16),
+            struct((ROWS, 9 * TRACE), bf16),
             struct((ROWS, 3 * TRACE), bf16),
             struct((TRACE, 3 * TRACE), bf16),
         ),
+        scratch_shapes=[
+            pltpu.VMEM((DEPTH, wide), f32),
+            pltpu.VMEM((PAD, DEPTH), f32),
+            pltpu.VMEM((DEPTH, DEPTH), f32),
+            pltpu.VMEM((count * ROWS, DEPTH), f32),
+            pltpu.VMEM((count * ROWS, DEPTH), f32),
+        ],
         cost_estimate=cost(1 << 24),
+        compiler_params=params,
         name="prepare",
-    )(strain_map, face_mass, mass_inverse, spread, rows, place, lift, lift0)
+    )(strain_map.T, face_mass, mass_inverse, place, lift, lift0)
+    ops = (strain_op, pick, lift_op)
 
     field, vel, coef, index, rim = pl.pallas_call(
         functools.partial(start_rim, sizes),
@@ -589,8 +645,9 @@
             struct((8, lanes), jnp.int32),
             struct((8, lanes)),
         ),
-        in_specs=[part, part] + [vmem] * 12,
+        in_specs=[part, part] + [vmem] * 11,
         cost_estimate=cost(1 << 24),
+        compiler_params=params,
         name="start_rim",
     )(
         displacement,
@@ -603,10 +660,7 @@
         neighbour_geometry,
         cross_row,
         cross_geometry,
-        high_op,
-        low_op,
-        pick,
-        lift_op,
+        *ops,
     )
 
     field, vel, own, rim, *sends = pl.pallas_call(
@@ -614,12 +668,14 @@
         out_shape=(state_shape, state_shape, struct((TRACE, lanes)), struct((8, lanes)))
         + messages(2 * TRACE),
         cost_estimate=cost(1 << 24),
+        compiler_params=params,
         name="first_step",
-    )(*arrived, field, vel, coef, index, rim, high_op, low_op, pick, lift_op, lift0_op)
+    )(*arrived, field, vel, coef, index, rim, *ops, lift0_op)
     arrived = exchange(*sends)
 
     inner = elements - lanes
     outputs = []
+    waits = []
     if inner:
         width = math.gcd(lanes, inner)
         skip = lanes // width
@@ -629,24 +685,29 @@
         def columns(height, q=0):
             return pl.BlockSpec((height, width), lambda i: (0, q * per_face + skip + i))
 
-        outputs = pl.pallas_call(
-            functools.partial(inside, 5),
+        def inner_columns(height):
+            return pl.BlockSpec((height, width), lambda i: (0, i))
+
+        inner_state = [
+            (ROWS, f32),
+            (ROWS, f32),
+            (24, f32),
+            (8, jnp.int32),
+        ]
+        state = pl.pallas_call(
+            functools.partial(inside_first, 3),
             grid=(inner // width,),
-            out_shape=(struct(displacement.shape), struct(displacement.shape)),
+            out_shape=[struct((height, inner), kind) for height, kind in inner_state],
             in_specs=[piece, piece]
             + [columns(2, q) for q in range(3)]
             + [columns(4, q) for q in range(3)]
             + [columns(count), columns(1)]
-            + [vmem] * 4,
-            out_specs=(piece, piece),
-            scratch_shapes=[
-                pltpu.VMEM((ROWS, width), f32),
-                pltpu.VMEM((ROWS, width), f32),
-                pltpu.VMEM((24, width), f32),
-                pltpu.VMEM((8, width), jnp.int32),
-            ],
+            + [vmem] * 3
+            + [anywhere],
+            out_specs=[inner_columns(height) for height, kind in inner_state],
             cost_estimate=cost(1 << 26),
-            name="inside",
+            compiler_params=params,
+            name="inside_first",
         )(
             displacement,
             velocity,
@@ -654,32 +715,48 @@
             *[local_geometry] * 3,
             geometry_weights,
             jac,
-            high_op,
-            low_op,
-            pick,
-            lift_op,
+            *ops,
+            own,
         )
+        waits = [state[0]]
 
     field, vel, own, *sends = pl.pallas_call(
         functools.partial(middle_steps, sizes),
         out_shape=(state_shape, state_shape, struct((TRACE, lanes))) + messages(2 * TRACE),
+        in_specs=[vmem] * 14 + [anywhere] * len(waits),
         cost_estimate=cost(1 << 24),
+        compiler_params=params,
         name="middle_steps",
-    )(*arrived, field, vel, own, coef, index, rim, high_op, low_op, pick, lift_op, lift0_op, trace_op)
+    )(*arrived, field, vel, own, coef, index, rim, *ops, lift0_op, trace_op, *waits)
     arrived = exchange(*sends)
 
-    anywhere = pl.BlockSpec(memory_space=pl.ANY)
+    if inner:
+        outputs = pl.pallas_call(
+            functools.partial(inside_last, 2),
+            grid=(inner // width,),
+            out_shape=(struct(displacement.shape), struct(displacement.shape)),
+            in_specs=[inner_columns(height) for height, kind in inner_state]
+            + [vmem] * 3
+            + [anywhere],
+            out_specs=(piece, piece),
+            scratch_shapes=[pltpu.VMEM((ROWS, width), f32), pltpu.VMEM((ROWS, width), f32)],
+            cost_estimate=cost(1 << 26),
+            compiler_params=params,
+            name="inside_last",
+        )(*state, *ops, own)
+
     return pl.pallas_call(
         functools.partial(last_steps, sizes),
         grid=(1,),
         out_shape=(struct(displacement.shape), struct(displacement.shape)),
-        in_specs=[vmem] * 15 + [anywhere] * len(outputs),
+        in_specs=[vmem] * 14 + [anywhere] * len(outputs),
         out_specs=(part, part),
         scratch_shapes=[pltpu.VMEM((ROWS, lanes), f32), pltpu.VMEM((ROWS, lanes), f32)],
-        input_output_aliases={15: 0, 16: 1} if inner else {},
+        input_output_aliases={14: 0, 15: 1} if inner else {},
         cost_estimate=cost(1 << 24),
+        compiler_params=params,
         name="last_steps",
-    )(*arrived, field, vel, own, coef, index, rim, high_op, low_op, pick, lift_op, lift0_op, trace_op, *outputs)
+    )(*arrived, field, vel, own, coef, index, rim, *ops, lift0_op, trace_op, *outputs)
 
 
 def solution(mesh):

time: 66.6 us -> 57.8 us (0.87)
  Pallas kernels: 33.4 us -> 16.9 us
  local copies, waits for them, and re-layouts: 2.88 us -> 10.2 us
  starting transfers between devices: 23.1 us -> 25.1 us
  waiting for transfers between devices: 5.76 us -> 4.07 us
    pallas_call x2 -> x3, Pallas kernels: 15.5 us -> 7.98 us  [the longest x1 3.29 us: shards(): pl.pallas_call(functools.partial(inside_first, 3), grid=(inner // width,)...]
    unnamed x33 -> x46, local copies, waits for them, and re-layouts: 2.88 us -> 10.2 us
    pallas_call x1, Pallas kernels: 3.45 us -> 1.09 us  [shards(): pl.pallas_call(functools.partial(start_rim, sizes), grid=(1,), out_shape=...]
    pallas_call x1, Pallas kernels: 5.04 us -> 3.03 us  [shards(): pl.pallas_call(functools.partial(middle_steps, sizes), out_shape=(state_s...]
    ppermute x6, waiting for transfers between devices: 4.64 us -> 2.68 us  [shifted(): return lax.ppermute(value, axis, pairs)]
    pallas_call x1, Pallas kernels: 3.83 us -> 1.9 us  [shards(): pl.pallas_call(functools.partial(first_step, sizes), out_shape=(state_sha...]
    all_to_all x3, starting transfers between devices: 15.8 us -> 17.7 us  [exchange(): mixed = lax.all_to_all(cross, ('group', 'sub'), 0, 0, tiled=True)]
    pallas_call x1, Pallas kernels: 3.84 us -> 2.09 us  [shards(): pl.pallas_call(functools.partial(last_steps, sizes), grid=(1,), out_shape...]
  transfers between devices with their start and end apart: 9 -> 9, of which waited for: 3 -> 4; matrix products, arithmetic and copies ran while one was open for 1% -> 0% of each run, Pallas kernels for 29% -> 16%
where the time goes in v2:
time: 57.8 us; the launch traced here: 57.1 us
  starting transfers between devices  25.1 us (43%)
  Pallas kernels  16.9 us (29%)
  local copies, waits for them, and re-layouts  10.2 us (18%)
  waiting for transfers between devices  4.07 us (7%)
  between operations  0.86 us (1%)
    all_to_all x3, starting transfers between devices, exchange(): mixed = lax.all_to_all(cross, ('group', 'sub'), 0, 0, tiled=True)  17.7 us
    unnamed x46, local copies, waits for them, and re-layouts  10.2 us
    ppermute x6, starting transfers between devices, shifted(): return lax.ppermute(value, axis, pairs)  7.33 us
    pallas_call x1, Pallas kernels, shards(): pl.pallas_call(functools.partial(inside_first, 3), grid=(inner // width,)...  3.29 us
    pallas_call x1, Pallas kernels, shards(): pl.pallas_call(functools.partial(middle_steps, sizes), out_shape=(state_s...  3.03 us
    pallas_call x1, Pallas kernels, shards(): pl.pallas_call(functools.partial(inside_last, 2), grid=(inner // width,),...  2.91 us
    ppermute x6, waiting for transfers between devices, shifted(): return lax.ppermute(value, axis, pairs)  2.68 us
    pallas_call x1, Pallas kernels, shards(): pl.pallas_call(functools.partial(last_steps, sizes), grid=(1,), out_shape...  2.09 us
  transfers between devices with their start and end apart: 9, of which 4 were waited for; matrix products, arithmetic and copies ran while one was open for 0% of the time, Pallas kernels for 16%

profile of v2, /device:TPU:0, one launch (start us, length us, event | category | flops | bytes accessed | tf_op | source)
XLA Modules:
  0.0 57.1 jit_solution(900290956398070517)
XLA Ops:
  0.6 0.0 copy-start
  0.6 1.0 %copy-done = f32[3,35,1024]{2,1,0:T(8,128)S(1)} copy-done((f32[3,35,1024]{2,1,0:T(8,128)S(1)}, f32[3,35,1024]{2,1,0:T(8,128)}, u32[]{:S(2)}) %copy-start) | copy-done | bytes 430104
  1.7 0.0 copy-start.15
  1.7 0.7 %copy-done.15 = f32[1024]{0:T(1024)S(1)} copy-done((f32[1024]{0:T(1024)S(1)}, f32[1024]{0:T(1024)}, u32[]{:S(2)}) %copy-start.15) | copy-done | bytes 4120
  2.4 0.0 copy-start.3
  2.4 0.8 %first_pack.1 = (f32[56,128]{1,0:T(8,128)S(1)}, f32[56,128]{1,0:T(8,128)S(1)}, f32[32,8,128]{2,1,0:T(8,128)}) custom-call(f32[3,35,1024]{2,1,0:T(8,128)S(1)} %copy-done, f32[1,1024]{1,0:T(1,128)S(1)} %bitcast.4), custom_call_target="tpu_custom_call" | custom-call | flops 1048576 | bytes 1048576 | tf_op jit(solution)/shard_map/first_pack/pallas_call | solution.py:605
  3.1 0.0 copy-start.1
  3.1 7.3 %all-to-all-start = ((f32[32,8,128]{2,1,0:T(8,128)}), f32[32,8,128]{2,1,0:T(8,128)S(1)}, u32[]{:S(2)}, u32[]{:S(2)}) async-start(f32[32,8,128]{2,1,0:T(8,128)} %get-tuple-element.35), calls=%async_computation | async-start | bytes 262144 | tf_op jit(solution)/shard_map/all_to_all | solution.py:564
  10.4 2.4 %collective-permute-start = (f32[56,128]{1,0:T(8,128)S(1)}, f32[56,128]{1,0:T(8,128)S(1)}, u32[]{:S(2)}, u32[]{:S(2)}) collective-permute-start(f32[56,128]{1,0:T(8,128)S(1)} %get-tuple-element.33), channel_id=1, source_target_pairs={{0,7},{1,0},{2,1},{3,2},{4,3},{5,4},{6,5},{7,6},{8,15},{9,8},{10,9... | collective-permute-start | bytes 86024 | tf_op jit(solution)/shard_map/ppermute | solution.py:560
  12.9 0.0 collective-permute-start.1
  12.9 0.0 copy-start.6
  12.9 1.0 %copy-done.6 = f32[630,105]{0,1:T(8,128)S(1)} copy-done((f32[630,105]{0,1:T(8,128)S(1)}, f32[630,105]{0,1:T(8,128)}, u32[]{:S(2)}) %copy-start.6) | copy-done | bytes 264624
  13.8 0.0 copy-start.7
  13.8 0.9 %copy-done.7 = f32[432,15]{1,0:T(8,128)S(1)} copy-done((f32[432,15]{1,0:T(8,128)S(1)}, f32[432,15]{1,0:T(8,128)}, u32[]{:S(2)}) %copy-start.7) | copy-done | bytes 25944
  14.8 0.0 copy-start.9
  14.8 0.9 %copy-done.9 = f32[120,144]{1,0:T(8,128)S(1)} copy-done((f32[120,144]{1,0:T(8,128)S(1)}, f32[120,144]{1,0:T(8,128)}, u32[]{:S(2)}) %copy-start.9) | copy-done | bytes 69144
  15.7 0.0 copy-start.10
  15.7 0.8 %copy-done.10 = f32[120,48]{1,0:T(8,128)S(1)} copy-done((f32[120,48]{1,0:T(8,128)S(1)}, f32[120,48]{1,0:T(8,128)}, u32[]{:S(2)}) %copy-start.10) | copy-done | bytes 23064
  16.5 0.0 copy-start.17
  16.5 0.7 %copy-done.17 = f32[35,35]{1,0:T(8,128)S(1)} copy-done((f32[35,35]{1,0:T(8,128)S(1)}, f32[35,35]{1,0:T(8,128)}, u32[]{:S(2)}) %copy-start.17) | copy-done | bytes 4924
  17.2 0.7 %copy-done.18 = f32[15,15]{1,0:T(8,128)S(1)} copy-done((f32[15,15]{1,0:T(8,128)S(1)}, f32[15,15]{1,0:T(8,128)}, u32[]{:S(2)}) %copy-start.18) | copy-done | bytes 924
  18.0 0.0 copy-start.19
  18.0 0.0 copy-start.20
  18.0 0.0 copy-start.22
  18.0 1.8 %prepare.1 = (bf16[720,384]{1,0:T(8,128)(2,1)S(1)}, bf16[120,432]{1,0:T(8,128)(2,1)S(1)}, bf16[120,144]{1,0:T(8,128)(2,1)S(1)}, bf16[48,144]{1,0:T(8,128)(2,1)S(1)}) custom-call(f32[105,630]{1,0:T(8,128)S(1)} %bitcast.3, f32[15,15]{1,0:T(8,128)S(1)} %copy-done.18, f32[35,35]{1,0:T(8,128)S(1)} %copy-done.17, f32[432,15]{1,0:T(8,128)S(1)} %copy-done.7, ...), custom_call_target="tpu_custom_call" | custom-call | flops 16777216 | bytes 1048576 | tf_op jit(solution)/shard_map/prepare/pallas_call | solution.py:617
  19.8 0.0 copy-start.16
  19.8 0.0 copy-start.21
  19.8 0.0 copy-done.3
  19.8 0.0 copy-done.1
  19.8 0.0 copy-done.2
  19.8 0.0 copy-done.4
  19.8 0.0 copy-done.5
  19.8 0.0 copy-done.8
  19.9 0.0 copy-done.19
  19.9 0.0 copy-done.20
  19.9 0.0 copy-done.22
  19.9 0.6 %copy-done.16 = f32[1024]{0:T(1024)S(1)} copy-done((f32[1024]{0:T(1024)S(1)}, f32[1024]{0:T(1024)}, u32[]{:S(2)}) %copy-start.16) | copy-done | bytes 4120
  20.5 0.0 copy-done.21
  20.5 1.1 %start_rim.1 = (f32[120,512]{1,0:T(8,128)S(1)}, f32[120,512]{1,0:T(8,128)S(1)}, f32[24,512]{1,0:T(8,128)S(1)}, s32[8,512]{1,0:T(8,128)S(1)}, f32[8,512]{1,0:T(8,128)S(1)}) custom-call(f32[3,35,1024]{2,1,0:T(8,128)S(1)} %copy-done.1, f32[3,35,1024]{2,1,0:T(8,128)S(1)} %copy-done.3, s32[2,3072]{1,0:T(2,128)S(1)} %copy-done.5, f32[4,3072]{1,0:T(4,128)S(1)} %copy-done.4, ...), custom_call_target="tpu_custom_call" | custom-call | flops 16777216 | bytes 1048576 | tf_op jit(solution)/shard_map/start_rim/pallas_call | solution.py:638
  21.6 0.0 collective-permute-done.upper_in
  21.6 0.0 collective-permute-done.1.lower_in
  21.6 0.0 all-to-all-done.cross_in
  21.6 1.9 %first_step.1 = (f32[120,512]{1,0:T(8,128)S(1)}, f32[120,512]{1,0:T(8,128)S(1)}, f32[48,512]{1,0:T(8,128)S(1)}, f32[8,512]{1,0:T(8,128)S(1)}, f32[96,128]{1,0:T(...) custom-call(f32[56,128]{1,0:T(8,128)S(1)} %collective-permute-done.upper_in, ...), custom_call_target="tpu_custom_call" | custom-call | flops 16777216 | bytes 1048576 | tf_op jit(solution)/shard_map/first_step/pallas_call | solution.py:666
  23.5 5.8 %all-to-all-start.1 = ((f32[32,8,128]{2,1,0:T(8,128)}), f32[32,8,128]{2,1,0:T(8,128)S(1)}, u32[]{:S(2)}, u32[]{:S(2)}) async-start(f32[32,8,128]{2,1,0:T(8,128)} %get-tuple-element.46), calls=%async_computation.1 | async-start | bytes 262144 | tf_op jit(solution)/shard_map/all_to_all | solution.py:564
  29.3 2.4 %collective-permute-start.2 = (f32[96,128]{1,0:T(8,128)}, f32[96,128]{1,0:T(8,128)S(1)}, u32[]{:S(2)}, u32[]{:S(2)}) collective-permute-start(f32[96,128]{1,0:T(8,128)} %get-tuple-element.44), channel_id=1, source_target_pairs={{0,7},{1,0},{2,1},{3,2},{4,3},{5,4},{6,5},{7,6},{8,15},{9,8},{10,9... | collective-permute-start | bytes 147464 | tf_op jit(solution)/shard_map/ppermute | solution.py:560
  31.8 0.0 collective-permute-start.3
  31.8 3.3 %inside_first.1 = (f32[120,512]{1,0:T(8,128)S(1)}, f32[120,512]{1,0:T(8,128)S(1)}, f32[24,512]{1,0:T(8,128)S(1)}, s32[8,512]{1,0:T(8,128)S(1)}) custom-call(f32[3,35,1024]{2,1,0:T(8,128)S(1)} %copy-done.1, f32[3,35,1024]{2,1,0:T(8,128)S(1)} %copy-done.3, s32[2,3072]{1,0:T(2,128)S(1)} %copy-done.5, s32[2,3072]{1,0:T(2,128)S(1)} %copy-done.5, ...), custom_call_target="tpu_custom_call" | custom-call | flops 67108864 | bytes 1048576 | tf_op jit(solution)/shard_map/inside_first/pallas_call | solution.py:697
  35.1 0.0 collective-permute-done.2.upper_in
  35.1 0.0 copy-start.11
  35.1 0.6 %copy-done.11 = f32[96,128]{1,0:T(8,128)} copy-done((f32[96,128]{1,0:T(8,128)}, f32[96,128]{1,0:T(8,128)S(1)}, u32[]{:S(2)}) %copy-start.11) | copy-done | bytes 49176
  35.7 1.0 %collective-permute-done.3.lower_in = f32[96,128]{1,0:T(8,128)S(1)} collective-permute-done((f32[96,128]{1,0:T(8,128)}, f32[96,128]{1,0:T(8,128)S(1)}, u32[]{:S(2)}, u32[]{:S(2)}) %collective-permute-start.3) | collective-permute-done | bytes 49184 | tf_op jit(solution)/shard_map/ppermute | solution.py:560
  36.7 0.6 %copy-done.13 = f32[96,128]{1,0:T(8,128)} copy-done((f32[96,128]{1,0:T(8,128)}, f32[96,128]{1,0:T(8,128)S(1)}, u32[]{:S(2)}) %copy-start.13) | copy-done | bytes 49176
  37.3 0.3 all-to-all-done.1.cross_in
  37.5 0.8 %copy-done.12 = f32[96,128]{1,0:T(8,128)S(1)} copy-done((f32[96,128]{1,0:T(8,128)S(1)}, f32[96,128]{1,0:T(8,128)}, u32[]{:S(2)}) %copy-start.12) | copy-done | bytes 49176
  38.3 0.8 %copy-done.14 = f32[96,128]{1,0:T(8,128)S(1)} copy-done((f32[96,128]{1,0:T(8,128)S(1)}, f32[96,128]{1,0:T(8,128)}, u32[]{:S(2)}) %copy-start.14) | copy-done | bytes 49176
  39.1 3.0 %middle_steps.1 = (f32[120,512]{1,0:T(8,128)S(1)}, f32[120,512]{1,0:T(8,128)S(1)}, f32[48,512]{1,0:T(8,128)S(1)}, f32[96,128]{1,0:T(8,128)S(1)}, f32[96,128]{1,0:T(8,128)S(1)}, /*index=5*/f32[32,8,128]{2,1,0:T(8,128)}) custom-call(f32[96,128]{1,0:T(8,128)S(1)} %copy-done.12, f32[96,128]{1,0:T(8,128)S(1)} %copy-done.14, ...), custom_call_target="tpu_custom_call" | custom-call | flops 16777216 | bytes 1048576 | tf_op jit(solution)/shard_map/middle_steps/pallas_call | solution.py:723
  42.2 4.6 %all-to-all-start.2 = ((f32[32,8,128]{2,1,0:T(8,128)}), f32[32,8,128]{2,1,0:T(8,128)S(1)}, u32[]{:S(2)}, u32[]{:S(2)}) async-start(f32[32,8,128]{2,1,0:T(8,128)} %get-tuple-element.55), calls=%async_computation.2 | async-start | bytes 262144 | tf_op jit(solution)/shard_map/all_to_all | solution.py:564
  46.8 2.4 %collective-permute-start.4 = (f32[96,128]{1,0:T(8,128)S(1)}, f32[96,128]{1,0:T(8,128)S(1)}, u32[]{:S(2)}, u32[]{:S(2)}) collective-permute-start(f32[96,128]{1,0:T(8,128)S(1)} %get-tuple-element.53), channel_id=1, source_target_pairs={{0,7},{1,0},{2,1},{3,2},{4,3},{5,4},{6,5},{7,6},{8,15},{9,8},{10,9... | collective-permute-start | bytes 147464 | tf_op jit(solution)/shard_map/ppermute | solution.py:560
  49.2 0.0 collective-permute-start.5
  49.2 2.9 %inside_last.1 = (f32[3,35,1024]{2,1,0:T(8,128)}, f32[3,35,1024]{2,1,0:T(8,128)}) custom-call(f32[120,512]{1,0:T(8,128)S(1)} %get-tuple-element.52.rest_0_.field_in, f32[120,512]{1,0:T(8,128)S(1)} %get-tuple-element.59.speed_in, f32[24,512]{1,0:T(8,128)S(1)} %get-tuple-element.60.coef, s32[8,512]{1,0:T(8,128)S(1)} %get-tuple-element.61.index, ...), custom_call_target="tpu_custom_call" | custom-call | flops 67108864 | bytes 1048576 | tf_op jit(solution)/shard_map/inside_last/pallas_call | solution.py:734
  52.1 0.0 collective-permute-done.4.upper_in
  52.1 1.7 %collective-permute-done.5.lower_in = f32[96,128]{1,0:T(8,128)S(1)} collective-permute-done((f32[96,128]{1,0:T(8,128)S(1)}, f32[96,128]{1,0:T(8,128)S(1)}, u32[]{:S(2)}, u32[]{:S(2)}) %collective-permute-start.5) | collective-permute-done | bytes 49184 | tf_op jit(solution)/shard_map/ppermute | solution.py:560
  53.8 1.1 %all-to-all-done.2.cross_in = f32[32,8,128]{2,1,0:T(8,128)S(1)} async-done(((f32[32,8,128]{2,1,0:T(8,128)}), f32[32,8,128]{2,1,0:T(8,128)S(1)}, u32[]{:S(2)}, u32[]{:S(2)}) %all-to-all-start.2) | async-done | bytes 131104 | tf_op jit(solution)/shard_map/all_to_all | solution.py:564
  55.0 2.1 %last_steps.1 = (f32[3,35,1024]{2,1,0:T(8,128)}, f32[3,35,1024]{2,1,0:T(8,128)}) custom-call(f32[96,128]{1,0:T(8,128)S(1)} %collective-permute-done.4.upper_in, f32[96,128]{1,0:T(8,128)S(1)} %collective-permute-done.5.lower_in, f32[32,8,128]{2,1,0:T(8,128)S(1)} %all-to-all-done.2.cross_in, ...), custom_call_target="tpu_custom_call", output_to_operand_aliasing={{0}: (14, {}), {1}: (15, {})} | custom-call | flops 16777216 | bytes 1048576 | tf_op jit(solution)/shard_map/last_steps/pallas_call | solution.py:748
  (8 shorter events, 0.0 us)
Async XLA Ops:
  0.6 1.0 %copy-start = (f32[3,35,1024]{2,1,0:T(8,128)S(1)}, f32[3,35,1024]{2,1,0:T(8,128)}, u32[]{:S(2)}) copy-start(f32[3,35,1024]{2,1,0:T(8,128)} %disp.5) | copy-start | bytes 1290244
  1.7 0.7 %copy-start.15 = (f32[1024]{0:T(1024)S(1)}, f32[1024]{0:T(1024)}, u32[]{:S(2)}) copy-start(f32[1024]{0:T(1024)} %param.20) | copy-start | bytes 12292
  2.4 17.4 %copy-start.3 = (f32[3,35,1024]{2,1,0:T(8,128)S(1)}, f32[3,35,1024]{2,1,0:T(8,128)}, u32[]{:S(2)}) copy-start(f32[3,35,1024]{2,1,0:T(8,128)} %vel.3) | copy-start | bytes 1290244
  3.1 16.7 %copy-start.1 = (f32[3,35,1024]{2,1,0:T(8,128)S(1)}, f32[3,35,1024]{2,1,0:T(8,128)}, u32[]{:S(2)}) copy-start(f32[3,35,1024]{2,1,0:T(8,128)} %disp.5) | copy-start | bytes 1290244
  3.1 18.5 %all-to-all-start = ((f32[32,8,128]{2,1,0:T(8,128)}), f32[32,8,128]{2,1,0:T(8,128)S(1)}, u32[]{:S(2)}, u32[]{:S(2)}) async-start(f32[32,8,128]{2,1,0:T(8,128)} %get-tuple-element.35), calls=%async_computation | async-start | bytes 262144 | tf_op jit(solution)/shard_map/all_to_all | solution.py:564
  10.4 11.1 %collective-permute-start = (f32[56,128]{1,0:T(8,128)S(1)}, f32[56,128]{1,0:T(8,128)S(1)}, u32[]{:S(2)}, u32[]{:S(2)}) collective-permute-start(f32[56,128]{1,0:T(8,128)S(1)} %get-tuple-element.33), channel_id=1, source_target_pairs={{0,7},{1,0},{2,1},{3,2},{4,3},{5,4},{6,5},{7,6},{8,15},{9,8},{10,9... | collective-permute-start | bytes 86024 | tf_op jit(solution)/shard_map/ppermute | solution.py:560
  12.9 8.7 %collective-permute-start.1 = (f32[56,128]{1,0:T(8,128)S(1)}, f32[56,128]{1,0:T(8,128)S(1)}, u32[]{:S(2)}, u32[]{:S(2)}) collective-permute-start(f32[56,128]{1,0:T(8,128)S(1)} %get-tuple-element.34), channel_id=1, source_target_pairs={{0,1},{1,2},{2,3},{3,4},{4,5},{5,6},{6,7},{7,0},{8,9},{9,10},{10,1... | collective-permute-start | bytes 86024 | tf_op jit(solution)/shard_map/ppermute | solution.py:560
  12.9 1.0 %copy-start.6 = (f32[630,105]{0,1:T(8,128)S(1)}, f32[630,105]{0,1:T(8,128)}, u32[]{:S(2)}) copy-start(f32[630,105]{0,1:T(8,128)} %param.21) | copy-start | bytes 793804
  13.8 0.9 %copy-start.7 = (f32[432,15]{1,0:T(8,128)S(1)}, f32[432,15]{1,0:T(8,128)}, u32[]{:S(2)}) copy-start(f32[432,15]{1,0:T(8,128)} %constant.8.clone.place) | copy-start | bytes 77764
  14.8 0.9 %copy-start.9 = (f32[120,144]{1,0:T(8,128)S(1)}, f32[120,144]{1,0:T(8,128)}, u32[]{:S(2)}) copy-start(f32[120,144]{1,0:T(8,128)} %constant.9.clone.lift) | copy-start | bytes 207364
  15.7 0.8 %copy-start.10 = (f32[120,48]{1,0:T(8,128)S(1)}, f32[120,48]{1,0:T(8,128)}, u32[]{:S(2)}) copy-start(f32[120,48]{1,0:T(8,128)} %constant.10.clone.lift0) | copy-start | bytes 69124
  16.5 0.7 %copy-start.17 = (f32[35,35]{1,0:T(8,128)S(1)}, f32[35,35]{1,0:T(8,128)}, u32[]{:S(2)}) copy-start(f32[35,35]{1,0:T(8,128)} %mass_inverse.1) | copy-start | bytes 14704
  17.2 0.7 %copy-start.18 = (f32[15,15]{1,0:T(8,128)S(1)}, f32[15,15]{1,0:T(8,128)}, u32[]{:S(2)}) copy-start(f32[15,15]{1,0:T(8,128)} %face_mass.1) | copy-start | bytes 2704
  17.9 1.9 %copy-start.2 = (bf16[144,256]{1,0:T(8,128)(2,1)S(1)}, bf16[144,256]{1,0:T(8,128)(2,1)}, u32[]{:S(2)}) copy-start(bf16[144,256]{1,0:T(8,128)(2,1)} %constant.12.pick) | copy-start | bytes 221188
  17.9 1.9 %copy-start.4 = (f32[4,3072]{1,0:T(4,128)S(1)}, f32[4,3072]{1,0:T(4,128)}, u32[]{:S(2)}) copy-start(f32[4,3072]{1,0:T(4,128)} %geo3.1) | copy-start | bytes 147460
  17.9 1.9 %copy-start.5 = (s32[2,3072]{1,0:T(2,128)S(1)}, s32[2,3072]{1,0:T(2,128)}, u32[]{:S(2)}) copy-start(s32[2,3072]{1,0:T(2,128)} %link3.1) | copy-start | bytes 73732
  17.9 1.9 %copy-start.8 = (f32[6,1024]{1,0:T(8,128)S(1)}, f32[6,1024]{1,0:T(8,128)}, u32[]{:S(2)}) copy-start(f32[6,1024]{1,0:T(8,128)} %weights.3) | copy-start | bytes 73732
  18.0 1.9 %copy-start.19 = (f32[8,128]{1,0:T(8,128)S(1)}, f32[8,128]{1,0:T(8,128)}, u32[]{:S(2)}) copy-start(f32[8,128]{1,0:T(8,128)} %next_geometry.1) | copy-start | bytes 12292
  18.0 1.9 %copy-start.20 = (f32[4,192]{1,0:T(4,128)S(1)}, f32[4,192]{1,0:T(4,128)}, u32[]{:S(2)}) copy-start(f32[4,192]{1,0:T(4,128)} %cross_geometry.1) | copy-start | bytes 9220
  18.0 1.9 %copy-start.22 = (s32[192]{0:T(256)S(1)}, s32[192]{0:T(256)}, u32[]{:S(2)}) copy-start(s32[192]{0:T(256)} %param.28) | copy-start | bytes 2308
  19.8 0.7 %copy-start.16 = (f32[1024]{0:T(1024)S(1)}, f32[1024]{0:T(1024)}, u32[]{:S(2)}) copy-start(f32[1024]{0:T(1024)} %param.20) | copy-start | bytes 12292
  19.8 0.7 %copy-start.21 = (s32[2,128]{1,0:T(2,128)S(1)}, s32[2,128]{1,0:T(2,128)}, u32[]{:S(2)}) copy-start(s32[2,128]{1,0:T(2,128)} %next_links.1) | copy-start | bytes 3076
  23.5 14.0 %all-to-all-start.1 = ((f32[32,8,128]{2,1,0:T(8,128)}), f32[32,8,128]{2,1,0:T(8,128)S(1)}, u32[]{:S(2)}, u32[]{:S(2)}) async-start(f32[32,8,128]{2,1,0:T(8,128)} %get-tuple-element.46), calls=%async_computation.1 | async-start | bytes 262144 | tf_op jit(solution)/shard_map/all_to_all | solution.py:564
  29.3 5.7 %collective-permute-start.2 = (f32[96,128]{1,0:T(8,128)}, f32[96,128]{1,0:T(8,128)S(1)}, u32[]{:S(2)}, u32[]{:S(2)}) collective-permute-start(f32[96,128]{1,0:T(8,128)} %get-tuple-element.44), channel_id=1, source_target_pairs={{0,7},{1,0},{2,1},{3,2},{4,3},{5,4},{6,5},{7,6},{8,15},{9,8},{10,9... | collective-permute-start | bytes 147464 | tf_op jit(solution)/shard_map/ppermute | solution.py:560
  31.8 4.9 %collective-permute-start.3 = (f32[96,128]{1,0:T(8,128)}, f32[96,128]{1,0:T(8,128)S(1)}, u32[]{:S(2)}, u32[]{:S(2)}) collective-permute-start(f32[96,128]{1,0:T(8,128)} %get-tuple-element.45), channel_id=1, source_target_pairs={{0,1},{1,2},{2,3},{3,4},{4,5},{5,6},{6,7},{7,0},{8,9},{9,10},{10,1... | collective-permute-start | bytes 147464 | tf_op jit(solution)/shard_map/ppermute | solution.py:560
  35.1 0.6 %copy-start.11 = (f32[96,128]{1,0:T(8,128)}, f32[96,128]{1,0:T(8,128)S(1)}, u32[]{:S(2)}) copy-start(f32[96,128]{1,0:T(8,128)S(1)} %collective-permute-done.2.upper_in) | copy-start | bytes 147460
  36.7 0.6 %copy-start.13 = (f32[96,128]{1,0:T(8,128)}, f32[96,128]{1,0:T(8,128)S(1)}, u32[]{:S(2)}) copy-start(f32[96,128]{1,0:T(8,128)S(1)} %collective-permute-done.3.lower_in) | copy-start | bytes 147460
  37.5 0.8 %copy-start.12 = (f32[96,128]{1,0:T(8,128)S(1)}, f32[96,128]{1,0:T(8,128)}, u32[]{:S(2)}) copy-start(f32[96,128]{1,0:T(8,128)} %copy-done.11) | copy-start | bytes 147460
  38.3 0.8 %copy-start.14 = (f32[96,128]{1,0:T(8,128)S(1)}, f32[96,128]{1,0:T(8,128)}, u32[]{:S(2)}) copy-start(f32[96,128]{1,0:T(8,128)} %copy-done.13) | copy-start | bytes 147460
  42.2 12.8 %all-to-all-start.2 = ((f32[32,8,128]{2,1,0:T(8,128)}), f32[32,8,128]{2,1,0:T(8,128)S(1)}, u32[]{:S(2)}, u32[]{:S(2)}) async-start(f32[32,8,128]{2,1,0:T(8,128)} %get-tuple-element.55), calls=%async_computation.2 | async-start | bytes 262144 | tf_op jit(solution)/shard_map/all_to_all | solution.py:564
  46.8 5.4 %collective-permute-start.4 = (f32[96,128]{1,0:T(8,128)S(1)}, f32[96,128]{1,0:T(8,128)S(1)}, u32[]{:S(2)}, u32[]{:S(2)}) collective-permute-start(f32[96,128]{1,0:T(8,128)S(1)} %get-tuple-element.53), channel_id=1, source_target_pairs={{0,7},{1,0},{2,1},{3,2},{4,3},{5,4},{6,5},{7,6},{8,15},{9,8},{10,9... | collective-permute-start | bytes 147464 | tf_op jit(solution)/shard_map/ppermute | solution.py:560
  49.2 4.6 %collective-permute-start.5 = (f32[96,128]{1,0:T(8,128)S(1)}, f32[96,128]{1,0:T(8,128)S(1)}, u32[]{:S(2)}, u32[]{:S(2)}) collective-permute-start(f32[96,128]{1,0:T(8,128)S(1)} %get-tuple-element.54), channel_id=1, source_target_pairs={{0,1},{1,2},{2,3},{3,4},{4,5},{5,6},{6,7},{7,0},{8,9},{9,10},{10,1... | collective-permute-start | bytes 147464 | tf_op jit(solution)/shard_map/ppermute | solution.py:560
